TPU v7x, 32 devices: a whole 2x2x4 slice. The times are simulated.
32 devices in a mesh: gx: 8 (over y, x, core), gy: 4 (over z).
Axes of the slice: x: 2, y: 2, z: 4, core: 2. Of those that a mesh axis runs over, the one named last changes fastest.
Arguments:
- rhs_conc: float32 [16, 64, 2048], P('gx', 'gy'), may hold values from -60 to 60
- rhs_pots: float32 [16, 64, 33], P('gx', 'gy'), may hold values from -60 to 60
- diffusion: float32 [16, 64, 32], P('gx', 'gy'), may hold values from 0.05 to 5
- exchange: float32 [16, 64, 32], P('gx', 'gy'), may hold values from 0.2 to 4
- slope: float32 [16, 64, 32], P('gx', 'gy'), may hold values from 0.1 to 1
Outputs:
- sol_conc: float32 [16, 64, 2048], P('gx', 'gy')
- sol_pots: float32 [16, 64, 33], P('gx', 'gy')
All inputs are finite; a program needn't handle non-finite values.
Results may differ from a plain program's by a relative error of at most 0.0003.
Values sent between devices are 32-bit elements; how exact they have to be, the bound alone decides.
A program may use at most 64 MiB of HBM per device.

v0:
```python
import functools

import jax
import jax.numpy as jnp
from jax import lax
from jax.experimental import pallas as pl
from jax.experimental.pallas import tpu as pltpu
from jax.sharding import PartitionSpec as P

ITERS = 10
LANES = 128
CHUNK = 16

node_cond = 1.0
plane_cond = 0.5
collector_cond = 2.0
epsilon = 1e-06
first_shift = 3.0
MESH = pl.DeviceIdType.MESH


def add(terms):
    terms = [t for t in terms if t is not None]
    while len(terms) > 1:
        pairs = [terms[k] + terms[k + 1] for k in range(0, len(terms) - 1, 2)]
        terms = pairs + ([terms[-1]] if len(terms) % 2 else [])
    return terms[0]


def two_columns(last, upper, gram, along1, along2, z11, z12, z22, shift, root, ramp):
    span = range(last + 1)

    def images_of_rest(cu):
        out = []
        for k in span:
            terms = [cu[i] * upper[i][k] for i in range(max(k - 1, 0), last)]
            if k == last:
                terms.append(cu[last] * shift)
            out.append(add(terms))
        return out

    h = [along1[i] + shift * gram[i][last] for i in span]
    cu = [-h[i] for i in span]
    cu[last] = shift - h[last]
    gu = [h[i] - add([h[k] * gram[i][k] for k in span]) for i in span]
    g1 = z11 + shift * along1[last] - add([h[k] * along1[k] for k in span])
    g2 = z12 + shift * along2[last] - add([h[k] * along2[k] for k in span])
    square = add([cu[i] * gu[i] for i in span] + [g1])
    height, inverse = root(ramp(square))
    col1 = h + [height]
    first = [c * inverse for c in cu]
    near = [g * inverse for g in gu]
    near1, near2 = g1 * inverse, g2 * inverse
    near_self = ramp(square) * inverse * inverse

    cw = [c * inverse for c in images_of_rest(cu)]
    c1 = (cu[last] + shift) * inverse
    c2 = inverse
    g = [
        add([cw[k] * gram[i][k] for k in span] + [c1 * along1[i], c2 * along2[i]]) for i in span
    ]
    g1 = add([cw[k] * along1[k] for k in span] + [c1 * z11, c2 * z12])
    g2 = add([cw[k] * along2[k] for k in span] + [c1 * z12, c2 * z22])
    h = list(g)
    top = add([first[i] * g[i] for i in span] + [inverse * g1])
    cu = [cw[i] - h[i] - top * first[i] for i in span]
    c1 = c1 - top * inverse
    gu = [g[i] - add([h[k] * gram[i][k] for k in span] + [top * near[i]]) for i in span]
    g1 = g1 - add([h[k] * along1[k] for k in span] + [top * near1])
    g2 = g2 - add([h[k] * along2[k] for k in span] + [top * near2])
    square = add([cu[i] * gu[i] for i in span] + [c1 * g1, c2 * g2])
    height, inverse2 = root(ramp(square))
    col2 = h + [top, height]
    second = ([c * inverse2 for c in cu], c1 * inverse2, c2 * inverse2)

    def next_image(new_shift):
        cq, d1, d2 = second
        out = images_of_rest(cq)
        out = [out[k] - new_shift * cq[k] for k in span]
        e1 = cq[last] + d1 * (shift - new_shift)
        e2 = d1 + d2 * (shift - new_shift)
        return out, e1, e2, d2

    gram = [list(gram[i]) + [near[i], gu[i] * inverse2] for i in span]
    cross = add([first[i] * gu[i] for i in span] + [inverse * g1]) * inverse2
    gram.append([gram[i][last + 1] for i in span] + [near_self, cross])
    gram.append([gram[i][last + 2] for i in span] + [cross, ramp(square) * inverse2 * inverse2])
    return col1, col2, (first, inverse), second, next_image, gram


def cycle(
    sizes,
    conc_ref,
    pots_ref,
    diff_ref,
    exch_ref,
    slope_ref,
    sol_conc_ref,
    sol_pots_ref,
    turned,
    basis,
    images,
    edges,
    halos,
    rows,
    sent_rows,
    edge_send,
    edge_recv,
    row_send,
    row_recv,
    load_sem,
):
    nx, ny = sizes
    count = nx * ny
    cx, cy = conc_ref.shape[0], conc_ref.shape[1]
    cells = cx * cy
    nodes = exch_ref.shape[2]
    shells = conc_ref.shape[2] // nodes
    groups = LANES // cells
    subs = nodes // groups
    mx = lax.axis_index("gx")
    my = lax.axis_index("gy")
    me = mx * ny + my

    def peers(act):
        if count <= 32:
            for dx in range(nx - 1, -1, -1):
                for dy in range(ny - 1, -1, -1):
                    if dx or dy:
                        act(lax.rem(mx + dx, nx), lax.rem(my + dy, ny))
        else:

            def one(p, carry):
                other = lax.rem(me + p, count)
                act(lax.div(other, ny), lax.rem(other, ny))
                return carry

            lax.fori_loop(1, count, one, 0)

    barrier = pltpu.get_barrier_semaphore()
    peers(
        lambda px, py: pl.semaphore_signal(
            barrier, inc=1, device_id={"gx": px, "gy": py}, device_id_type=MESH
        )
    )

    span = subs * shells
    loads = []
    for x in range(cx):
        for g in range(groups):
            edge_row = g * cells + x * cy
            loads.append(
                pltpu.make_async_copy(
                    conc_ref.at[x, :, g * span : (g + 1) * span],
                    turned.at[edge_row : edge_row + cy, :],
                    load_sem.at[x, g],
                )
            )
    for copy in loads:
        copy.start()

    def fold_nodes(block):
        flat = block.reshape(cells, block.shape[2])
        return flat.T

    def node_register(flat_t):
        return jnp.concatenate(
            [flat_t[g * subs : (g + 1) * subs, :] for g in range(groups)], axis=1
        )

    diff = node_register(fold_nodes(diff_ref[...]))
    exch = node_register(fold_nodes(exch_ref[...]))
    slope = node_register(fold_nodes(slope_ref[...]))
    pots_t = fold_nodes(pots_ref[...])
    pot = node_register(pots_t)
    vol_row = pots_t[nodes : nodes + 1, :]
    vol = jnp.broadcast_to(jnp.concatenate([vol_row] * groups, axis=1), (subs, LANES))

    for copy in loads:
        copy.wait()
    turned_t = turned[...].T.reshape(subs, shells, LANES)
    for s in range(subs):
        images[2, 1 : shells + 1, s, :] = turned_t[s]

    lane = lax.broadcasted_iota(jnp.int32, (subs, LANES), 1)
    sub = lax.broadcasted_iota(jnp.int32, (subs, LANES), 0)
    group = lane // cells
    cell = lane % cells
    cell_x = cell // cy
    cell_y = cell % cy
    single = ((sub == 0) & (group == 0)).astype(jnp.float32)
    first_sub, last_sub = sub == 0, sub == subs - 1
    first_group, last_group = group == 0, group == groups - 1
    inside_low_x, inside_high_x = cell_x > 0, cell_x < cx - 1
    inside_low_y, inside_high_y = cell_y > 0, cell_y < cy - 1
    zero = jnp.zeros((subs, LANES), jnp.float32)
    has = [mx > 0, mx < nx - 1, my > 0, my < ny - 1]
    goes = [has[1], has[0], has[3], has[2]]

    def roll(value, shift, axis=1):
        shift = shift % value.shape[axis]
        return pltpu.roll(value, shift, axis) if shift else value

    def inner_plane(p):
        return (
            4.0 * p
            - jnp.where(inside_low_x, roll(p, cy), zero)
            - jnp.where(inside_high_x, roll(p, -cy), zero)
            - jnp.where(inside_low_y, roll(p, 1), zero)
            - jnp.where(inside_high_y, roll(p, -1), zero)
        )

    def edge_sum(slot, member):
        low_x = roll(halos[slot, 0, member], -(cx - 1) * cy)
        high_x = roll(halos[slot, 1, member], (cx - 1) * cy)
        low_y = roll(halos[slot, 2, member], -(cy - 1))
        high_y = roll(halos[slot, 3, member], cy - 1)
        return (
            jnp.where(~inside_low_x & has[0], low_x, zero)
            + jnp.where(~inside_high_x & has[1], high_x, zero)
            + jnp.where(~inside_low_y & has[2], low_y, zero)
            + jnp.where(~inside_high_y & has[3], high_y, zero)
        )

    def node_mirror(p):
        low = roll(p, 1, 0)
        inner = jnp.where(first_sub, jnp.where(first_group, p, roll(low, cells)), low)
        high = roll(p, -1, 0)
        outer = jnp.where(last_sub, jnp.where(last_group, p, roll(high, -cells)), high)
        return 2.0 * p - inner - outer

    def node_mean(value):
        total = jnp.broadcast_to(jnp.sum(value, axis=0, keepdims=True), (subs, LANES))
        shift = cells
        while shift < LANES:
            total = total + roll(total, shift)
            shift *= 2
        return total * (1.0 / nodes)

    def edge_copies(slot):
        copies = []
        targets = [
            (lax.rem(mx + 1, nx), my),
            (lax.rem(mx + nx - 1, nx), my),
            (mx, lax.rem(my + 1, ny)),
            (mx, lax.rem(my + ny - 1, ny)),
        ]
        for k, (px, py) in enumerate(targets):
            copies.append(
                pltpu.make_async_remote_copy(
                    src_ref=edges.at[slot],
                    dst_ref=halos.at[slot, k],
                    send_sem=edge_send.at[slot, k],
                    recv_sem=edge_recv.at[slot, k],
                    device_id={"gx": px, "gy": py},
                    device_id_type=MESH,
                )
            )
        return copies

    def pots_image(vec, surface, shift):
        p, v, ep, ev = vec
        current = exch * (p - v)
        new_p = (
            node_cond * node_mirror(p)
            + current
            - slope * surface
            + plane_cond * (inner_plane(p) - ep)
        )
        new_v = collector_cond * (inner_plane(v) - ev) - node_mean(current)
        return new_p - shift * p, new_v - shift * v, current

    def shells_image(source, target, current, shift, dots=None, starts=()):
        images[source, 0] = images[source, 1]
        images[source, shells + 1] = images[source, shells]
        keep = (1.0 - shift)[None]

        def part(at, carry, last):
            here = images[source, pl.ds(at + 1, CHUNK)]
            low = images[source, pl.ds(at, CHUNK)]
            high = images[source, pl.ds(at + 2, CHUNK)]
            new = keep * here + diff[None] * (2.0 * here - low - high)
            if last:
                new = jnp.concatenate([new[:-1], new[-1:] + current[None]], axis=0)
            images[target, pl.ds(at + 1, CHUNK)] = new
            return tuple(dots(at, here, new, carry)) if dots else carry

        parts = shells // CHUNK
        carry = lax.fori_loop(
            0, parts - 1, lambda c, carry: part(c * CHUNK, carry, False), tuple(starts)
        )
        return part((parts - 1) * CHUNK, carry, True)

    def row_copy(step, px, py):
        return pltpu.make_async_remote_copy(
            src_ref=sent_rows.at[step],
            dst_ref=rows.at[step, me],
            send_sem=row_send.at[step],
            recv_sem=row_recv.at[step],
            device_id={"gx": px, "gy": py},
            device_id_type=MESH,
        )

    def send_dots(step, dots):
        padded = -(-len(dots) // 8) * 8
        stacked = [jnp.sum(d, axis=0, keepdims=True) for d in dots]
        stacked += [zero[:1]] * (padded - len(dots))
        tall = jnp.sum(jnp.concatenate(stacked, axis=0), axis=1, keepdims=True)
        at_row = lax.broadcasted_iota(jnp.int32, (padded, LANES), 0)
        at_lane = lax.broadcasted_iota(jnp.int32, (padded, LANES), 1)
        row = jnp.sum(jnp.where(at_row == at_lane, tall, 0.0), axis=0, keepdims=True)
        sent_rows[step] = row
        rows[step, me] = row
        peers(lambda px, py: row_copy(step, px, py).start())

    def wait_rows(step):
        part = rows.at[step, pl.ds(0, count - 1)]
        pltpu.make_async_copy(part, part, row_recv.at[step]).wait()

    def take_dots(step, wanted):
        total = jnp.sum(rows[step], axis=0)
        return [jnp.broadcast_to(total[:, k : k + 1], (subs, LANES)) for k in range(wanted)]

    pending = []

    def send_edges(slot, p, v):
        edges[slot, 0] = p
        edges[slot, 1] = v
        copies = edge_copies(slot)
        for copy, there in zip(copies, goes):
            pl.when(there)(copy.start)
        pending.append(copies)
        return copies

    def take_edges(slot, copies, p, v):
        for copy, there in zip(copies, has):
            pl.when(there)(copy.wait_recv)
        return p, v, edge_sum(slot, 0), edge_sum(slot, 1)

    def root(square):
        height = jnp.sqrt(square + epsilon)
        return height, 1.0 / height

    def ramp(square):
        return jnp.maximum(square, 0.0)

    def combine(coeffs, members):
        return add([c * m for c, m in zip(coeffs, members)])

    columns, cosines, sines, uppers, target = [], [], [], [], []

    def rotate():
        for step in range(len(uppers), len(columns)):
            entries = list(columns[step])
            for row in range(step):
                first = cosines[row] * entries[row] + sines[row] * entries[row + 1]
                second = cosines[row] * entries[row + 1] - sines[row] * entries[row]
                entries[row] = first
                entries[row + 1] = second
            square = entries[step] * entries[step] + entries[step + 1] * entries[step + 1]
            radius = jnp.sqrt(square)
            cosine = entries[step] / radius
            sine = entries[step + 1] / radius
            entries[step] = radius
            cosines.append(cosine)
            sines.append(sine)
            lead = target[step]
            target[step] = cosine * lead
            target.append(-sine * lead)
            uppers.append(entries[: step + 1])

    shift = jnp.full((subs, LANES), first_shift, jnp.float32)
    images_pots = [None, None, None]
    pl.semaphore_wait(barrier, count - 1)
    copies = send_edges(0, pot, vol)
    vecs = [take_edges(0, copies, pot, vol)]
    p, v, current = pots_image(vecs[0], images[2, shells], shift)
    copies = send_edges(1, p, v)

    def keep_first(at, here, new, carry):
        basis[0, pl.ds(at, CHUNK)] = here
        return carry

    shells_image(2, 0, current, shift, keep_first)
    images_pots[0] = take_edges(1, copies, p, v)
    p, v, current = pots_image(images_pots[0], images[0, shells], shift)
    slot = 2
    copies = send_edges(slot, p, v)
    gram = None
    for last in range(0, ITERS, 2):
        block = last // 2
        more = last + 2 < ITERS
        v_once = v * single
        z1 = images_pots[0]
        z1_once = z1[1] * single
        starts = [vecs[i][0] * z1[0] + vecs[i][1] * z1_once for i in range(last + 1)]
        starts += [vecs[i][0] * p + vecs[i][1] * v_once for i in range(last + 1)]
        starts += [z1[0] * z1[0] + z1[1] * z1_once]
        starts += [z1[0] * p + z1[1] * v_once, p * p + v * v_once]
        if block == 0:
            starts.append(pot * pot + vol * (vol * single))

        def dots(at, here, new, carry):
            others = [basis[i, pl.ds(at, CHUNK)] for i in range(last + 1)]
            out = [jnp.sum(q * here, axis=0) for q in others]
            out += [jnp.sum(q * new, axis=0) for q in others]
            out += [jnp.sum(m * n, axis=0) for m, n in ((here, here), (here, new), (new, new))]
            if block == 0:
                out.append(jnp.sum(others[0] * others[0], axis=0))
            return [c + o for c, o in zip(carry, out)]

        products = shells_image(0, 1, current, shift, dots, starts)
        send_dots(block, products)
        rotate()
        if more:
            images_pots[1] = take_edges(slot, copies, p, v)
            p, v, current = pots_image(images_pots[1], images[1, shells], shift)
            slot += 1
            copies = send_edges(slot, p, v)
            shells_image(1, 2, current, shift)
        wait_rows(block)
        sums = take_dots(block, len(products))
        scale = None
        if block == 0:
            beta, scale = root(sums[5])
            target.append(beta)
            sums = [s * scale * scale for s in sums]
            gram = [[sums[5]]]
        width = last + 1
        col1, col2, first, second, next_image, gram = two_columns(
            last,
            columns,
            gram,
            sums[:width],
            sums[width : 2 * width],
            sums[2 * width],
            sums[2 * width + 1],
            sums[2 * width + 2],
            shift,
            root,
            ramp,
        )
        columns += [col1, col2]
        if not more:
            break
        new_shift = col1[last]
        along, e1, e2, e3 = next_image(new_shift)
        one = first[0] + [first[1]]
        two = second[0] + [second[1], second[2]]
        three = along + [e1, e2, e3]
        shift = new_shift
        if block == 0:
            one, two, three = ([c * scale for c in cs] for cs in (one, two, three))
        images_pots[2] = take_edges(slot, copies, p, v)
        members = [list(m) for m in zip(*(vecs + images_pots))]
        new_vecs = [tuple(combine(cs, m) for m in members) for cs in (one, two, three)]
        if block == 0:
            vecs[0] = tuple(m * scale for m in vecs[0])
        vecs += new_vecs[:2]
        images_pots = [new_vecs[2], None, None]
        surfaces = [basis[i, shells - 1] for i in range(width)] + [
            images[k, shells] for k in range(3)
        ]
        p, v, current = pots_image(images_pots[0], combine(three, surfaces), shift)
        if last + 4 < ITERS:
            slot += 1
            copies = send_edges(slot, p, v)

        def advance(c, carry):
            at = c * CHUNK
            parts = [basis[i, pl.ds(at, CHUNK)] for i in range(width)]
            parts += [images[k, pl.ds(at + 1, CHUNK)] for k in range(3)]
            basis[last + 1, pl.ds(at, CHUNK)] = combine(one, parts)
            basis[last + 2, pl.ds(at, CHUNK)] = combine(two, parts)
            images[0, pl.ds(at + 1, CHUNK)] = combine(three, parts)
            if block == 0:
                basis[0, pl.ds(at, CHUNK)] = parts[0] * scale
            return carry

        lax.fori_loop(0, shells // CHUNK, advance, 0)
    rotate()

    weights = [None] * ITERS
    for row in range(ITERS - 1, -1, -1):
        total = target[row]
        for later in range(ITERS - 1, row, -1):
            total = total - uppers[later][row] * weights[later]
        weights[row] = total * (1.0 / uppers[row][row])
    tail = weights[ITERS - 1]
    mixed = [weights[i] + tail * first[0][i] for i in range(ITERS - 1)] + [tail * first[1]]

    sol_p = combine(mixed, [m[0] for m in vecs] + [images_pots[0][0]])
    sol_v = combine(mixed, [m[1] for m in vecs] + [images_pots[0][1]])

    def gather(c, carry):
        at = c * CHUNK
        parts = [basis[i, pl.ds(at, CHUNK)] for i in range(ITERS - 1)]
        parts.append(images[0, pl.ds(at + 1, CHUNK)])
        images[1, pl.ds(at + 1, CHUNK)] = combine(mixed, parts)
        return carry

    lax.fori_loop(0, shells // CHUNK, gather, 0)
    flat = jnp.concatenate([images[1, 1 : shells + 1, s, :] for s in range(subs)], axis=0)
    turned[...] = flat.T
    for x in range(cx):
        for g in range(groups):
            edge_row = g * cells + x * cy
            sol_conc_ref[x, :, g * span : (g + 1) * span] = turned[edge_row : edge_row + cy, :]
    flat_p = jnp.concatenate(
        [sol_p[:, g * cells : (g + 1) * cells] for g in range(groups)] + [sol_v[:1, :cells]], axis=0
    )
    sol_pots_ref[...] = flat_p.T.reshape(cx, cy, nodes + 1)

    for copies in pending:
        for copy, there in zip(copies, goes):
            pl.when(there)(copy.wait_send)
    for step in range(ITERS // 2):
        part = rows.at[step, pl.ds(0, count - 1)]
        pltpu.make_async_copy(part, part, row_send.at[step]).wait()


def solution(mesh):
    sizes = (mesh.shape["gx"], mesh.shape["gy"])
    count = sizes[0] * sizes[1]

    def shards(rhs_conc, rhs_pots, diffusion, exchange, slope):
        cells = rhs_conc.shape[0] * rhs_conc.shape[1]
        nodes = exchange.shape[2]
        shells = rhs_conc.shape[2] // nodes
        groups = LANES // cells
        subs = nodes // groups
        vmem = pl.BlockSpec(memory_space=pltpu.VMEM)
        return pl.pallas_call(
            functools.partial(cycle, sizes),
            out_shape=(
                jax.ShapeDtypeStruct(rhs_conc.shape, jnp.float32),
                jax.ShapeDtypeStruct(rhs_pots.shape, jnp.float32),
            ),
            in_specs=[pl.BlockSpec(memory_space=pl.ANY)] + [vmem] * 4,
            out_specs=(vmem, vmem),
            scratch_shapes=[
                pltpu.VMEM((LANES, subs * shells), jnp.float32),
                pltpu.VMEM((ITERS - 1, shells, subs, LANES), jnp.float32),
                pltpu.VMEM((3, shells + 2, subs, LANES), jnp.float32),
                pltpu.VMEM((ITERS, 2, subs, LANES), jnp.float32),
                pltpu.VMEM((ITERS, 4, 2, subs, LANES), jnp.float32),
                pltpu.VMEM((ITERS // 2, count, 1, LANES), jnp.float32),
                pltpu.VMEM((ITERS // 2, 1, LANES), jnp.float32),
                pltpu.SemaphoreType.DMA((ITERS, 4)),
                pltpu.SemaphoreType.DMA((ITERS, 4)),
                pltpu.SemaphoreType.DMA((ITERS // 2,)),
                pltpu.SemaphoreType.DMA((ITERS // 2,)),
                pltpu.SemaphoreType.DMA((rhs_conc.shape[0], groups)),
            ],
            compiler_params=pltpu.CompilerParams(collective_id=0, has_side_effects=True),
        )(rhs_conc, rhs_pots, diffusion, exchange, slope)

    spec = P("gx", "gy", None)
    return jax.shard_map(
        shards,
        mesh=mesh,
        in_specs=(spec,) * 5,
        out_specs=(spec, spec),
        check_vma=False,
    )
```

profile of v0, /device:TPU:0, one launch (start us, length us, event | category | flops | bytes accessed | tf_op | source)
XLA Modules:
  0.0 46.7 jit_solution(7032890055204663286)
XLA Ops:
  0.6 43.8 %shard_map.68 = (f32[2,16,2048]{2,1,0:T(8,128)}, f32[2,16,33]{2,1,0:T(8,128)}) custom-call(f32[2,16,2048]{2,1,0:T(8,128)} %conc_ref.1, f32[2,16,33]{2,1,0:T(8,128)} %pots_ref.1, f32[2,16,32]{2,1,0:T(8,128)} %diff_ref.1, f32[2,16,32]{2,1,0:T(8,128)} %exch_ref.1, f32[2,16,32]{2,1,0:T(8,128)} %slope_ref.1), custom_call_target="tpu_custom_call" | custom-call | tf_op jit(solution)/shard_map/pallas_call | solution.py:533
  44.5 0.0 copy-start
  44.5 1.7 %copy.9 = f32[2,16,2048]{2,1,0:T(8,128)} copy(f32[2,16,2048]{2,1,0:T(8,128)} %get-tuple-element.4) | data formatting | bytes 524288
  46.1 0.0 copy-done
  46.1 0.6 %copy.10 = f32[2,16,33]{2,1,0:T(8,128)} copy(f32[2,16,33]{2,1,0:T(8,128)S(1)} %copy-done) | data formatting | bytes 8448
Async XLA Ops:
  44.5 1.7 %copy-start = (f32[2,16,33]{2,1,0:T(8,128)S(1)}, f32[2,16,33]{2,1,0:T(8,128)}, u32[]{:S(2)}) copy-start(f32[2,16,33]{2,1,0:T(8,128)} %get-tuple-element.5) | copy-start | bytes 12676
where the time goes:
time: 47.1 us; the launch traced here: 46.7 us
  Pallas kernels  43.8 us (93%)
  local copies, waits for them, and re-layouts  2.28 us (5%)
  between operations  0.65 us (1%)
    pallas_call x1, Pallas kernels, shards(): pl.pallas_call(functools.partial(cycle, sizes), out_shape=(jax.ShapeDtype...  43.8 us
    unnamed x4, local copies, waits for them, and re-layouts  2.28 us

commit v1 on v0

v1 whole, which is shorter than its diff:
```python
import functools

import jax
import jax.numpy as jnp
from jax import lax
from jax.experimental import pallas as pl
from jax.experimental.pallas import tpu as pltpu
from jax.sharding import PartitionSpec as P

ITERS = 10
LANES = 128
CHUNK = 16
PLAN = (2, 2, 2, 2, 2)
ADAPTIVE = 2

node_cond = 1.0
plane_cond = 0.5
collector_cond = 2.0
epsilon = 1e-06
center = 10.0
radius = 10.0
least_height = 0.05
least_pivot = 3e-07
MESH = pl.DeviceIdType.MESH


def add(terms):
    terms = [t for t in terms if t is not None]
    while len(terms) > 1:
        pairs = [terms[k] + terms[k + 1] for k in range(0, len(terms) - 1, 2)]
        terms = pairs + ([terms[-1]] if len(terms) % 2 else [])
    return terms[0]


def factor(gram):
    size = len(gram)
    left = [[gram[i][j] for j in range(size)] for i in range(size)]
    upper = [[None] * size for _ in range(size)]
    inverse = []
    for k in range(size):
        pivot = left[k][k]
        good = pivot > least_pivot * gram[k][k]
        inv = jnp.where(good, lax.rsqrt(jnp.where(good, pivot, 1.0)), 0.0)
        inverse.append(inv)
        upper[k][k] = pivot * inv
        for j in range(k + 1, size):
            upper[k][j] = left[k][j] * inv
        for i in range(k + 1, size):
            for j in range(i, size):
                left[i][j] = left[i][j] - upper[k][i] * upper[k][j]
    return upper, inverse


def project(upper, inverse, recurrence):
    columns = []
    for k, (alpha, gamma, beta) in enumerate(recurrence):
        column = []
        for i in range(k + 2):
            terms = [beta * upper[i][k + 1]]
            if i <= k:
                terms.append(alpha * upper[i][k])
            if i <= k - 1 and gamma is not None:
                terms.append(gamma * upper[i][k - 1])
            value = add(terms)
            known = [columns[m][i] * upper[m][k] for m in range(max(i - 1, 0), k)]
            if known:
                value = value - add(known)
            column.append(value * inverse[k])
        columns.append(column)
    return columns


def arnoldi(upper, inverse, images, count):
    height = jnp.sqrt(upper[0][0] * upper[0][0] + epsilon)
    start = height
    vectors = [[upper[0][0] / height]]
    columns = []
    for j in range(count):
        newest = vectors[j]
        image = [
            add([images[k][t] * newest[k] for k in range(max(t - 1, 0), j + 1)])
            for t in range(j + 2)
        ]
        coeffs = [
            add([vectors[i][t] * image[t] for t in range(i + 1)]) for i in range(j + 1)
        ]
        rest = [
            image[t] - add([coeffs[i] * vectors[i][t] for i in range(t, j + 1)])
            for t in range(j + 1)
        ] + [image[j + 1]]
        height = jnp.sqrt(add([r * r for r in rest]) + epsilon)
        columns.append(coeffs + [height])
        if j + 1 < count:
            scale = 1.0 / height
            vectors.append([r * scale for r in rest])
    return start, vectors, columns


def least_squares(columns, start):
    target, cosines, sines, uppers = [start], [], [], []
    for step, column in enumerate(columns):
        entries = list(column)
        for row in range(step):
            first = cosines[row] * entries[row] + sines[row] * entries[row + 1]
            second = cosines[row] * entries[row + 1] - sines[row] * entries[row]
            entries[row] = first
            entries[row + 1] = second
        size = jnp.sqrt(entries[step] * entries[step] + entries[step + 1] * entries[step + 1])
        shrink = 1.0 / size
        cosine = entries[step] * shrink
        sine = entries[step + 1] * shrink
        entries[step] = size
        cosines.append(cosine)
        sines.append(sine)
        lead = target[step]
        target[step] = cosine * lead
        target.append(-sine * lead)
        uppers.append((entries[: step + 1], shrink))
    weights = [None] * len(columns)
    for row in range(len(columns) - 1, -1, -1):
        total = target[row]
        for later in range(len(columns) - 1, row, -1):
            total = total - uppers[later][0][row] * weights[later]
        weights[row] = total * uppers[row][1]
    return weights


def expand(weights, vectors, upper, inverse):
    count = len(weights)
    along = [add([vectors[j][t] * weights[j] for j in range(t, count)]) for t in range(count)]
    out = [None] * count
    for row in range(count - 1, -1, -1):
        total = along[row]
        for later in range(count - 1, row, -1):
            total = total - upper[row][later] * out[later]
        out[row] = total * inverse[row]
    return out


def surroundings(cx, cy, depth):
    def away(extent, offset):
        return (abs(offset) - 1) * extent + 1 if offset else 0

    found = {}
    for a in range(-depth, depth + 1):
        for b in range(-depth, depth + 1):
            distance = away(cx, a) + away(cy, b)
            if 0 < distance <= depth:
                found[a, b] = distance
    return found


def cycle(
    sizes,
    conc_ref,
    pots_ref,
    diff_ref,
    exch_ref,
    slope_ref,
    sol_conc_ref,
    sol_pots_ref,
    turned,
    basis,
    raw_pots,
    raw_fixed,
    sent,
    halos,
    fixed_sent,
    fixed_halos,
    rows,
    sent_rows,
    edge_send,
    edge_recv,
    fixed_send,
    fixed_recv,
    row_send,
    row_recv,
    load_sem,
    small_sem,
    out_sem,
):
    nx, ny = sizes
    count = nx * ny
    cx, cy = conc_ref.shape[0], conc_ref.shape[1]
    cells = cx * cy
    nodes = exch_ref.shape[2]
    shells = conc_ref.shape[2] // nodes
    groups = LANES // cells
    subs = nodes // groups
    mx = lax.axis_index("gx")
    my = lax.axis_index("gy")
    me = mx * ny + my
    deepest = max(PLAN)
    around = surroundings(cx, cy, deepest)
    order = sorted(around, key=lambda o: -around[o])
    place = {o: i for i, o in enumerate(order)}

    def peers(act):
        if count <= 32:
            for dx in range(nx - 1, -1, -1):
                for dy in range(ny - 1, -1, -1):
                    if dx or dy:
                        act(lax.rem(mx + dx, nx), lax.rem(my + dy, ny))
        else:

            def one(p, carry):
                other = lax.rem(me + p, count)
                act(lax.div(other, ny), lax.rem(other, ny))
                return carry

            lax.fori_loop(1, count, one, 0)

    barrier = pltpu.get_barrier_semaphore()
    peers(
        lambda px, py: pl.semaphore_signal(
            barrier, inc=1, device_id={"gx": px, "gy": py}, device_id_type=MESH
        )
    )

    span = subs * shells
    loads = []
    for x in range(cx):
        for g in range(groups):
            edge_row = g * cells + x * cy
            loads.append(
                pltpu.make_async_copy(
                    conc_ref.at[x, :, g * span : (g + 1) * span],
                    turned.at[edge_row : edge_row + cy, :],
                    load_sem.at[x, g],
                )
            )
    small = [pltpu.make_async_copy(pots_ref, raw_pots, small_sem.at[0])]
    for k, ref in enumerate((exch_ref, slope_ref, diff_ref)):
        small.append(pltpu.make_async_copy(ref, raw_fixed.at[k], small_sem.at[k + 1]))
    for copy in small + loads:
        copy.start()
    for copy in small:
        copy.wait()

    def fold_nodes(block):
        return block.reshape(cells, block.shape[2]).T

    def node_register(flat_t):
        return jnp.concatenate(
            [flat_t[g * subs : (g + 1) * subs, :] for g in range(groups)], axis=1
        )

    exch = node_register(fold_nodes(raw_fixed[0]))
    slope = node_register(fold_nodes(raw_fixed[1]))
    diff = node_register(fold_nodes(raw_fixed[2]))
    pots_t = fold_nodes(raw_pots[...])
    pot = node_register(pots_t)
    vol_row = pots_t[nodes : nodes + 1, :]
    vol = jnp.broadcast_to(jnp.concatenate([vol_row] * groups, axis=1), (subs, LANES))
    for k, value in enumerate((exch, slope, diff)):
        fixed_sent[k] = value

    lane = lax.broadcasted_iota(jnp.int32, (subs, LANES), 1)
    sub = lax.broadcasted_iota(jnp.int32, (subs, LANES), 0)
    group = lane // cells
    cell = lane % cells
    cell_x = cell // cy
    cell_y = cell % cy
    single = ((sub == 0) & (group == 0)).astype(jnp.float32)
    first_sub, last_sub = sub == 0, sub == subs - 1
    first_group, last_group = group == 0, group == groups - 1
    low_x, high_x = cell_x == 0, cell_x == cx - 1
    low_y, high_y = cell_y == 0, cell_y == cy - 1
    zero = jnp.zeros((subs, LANES), jnp.float32)

    there = {}
    for a, b in order:
        there[a, b] = (
            (mx + a >= 0) & (mx + a < nx) & (my + b >= 0) & (my + b < ny)
        )

    def roll(value, shift, axis=1):
        shift = shift % value.shape[axis]
        return pltpu.roll(value, shift, axis) if shift else value

    def sides(p, low_block, high_block, edge_low, edge_high, step, wide):
        low = roll(p, step)
        low = jnp.where(edge_low, zero if low_block is None else roll(low_block, -wide), low)
        high = roll(p, -step)
        high = jnp.where(edge_high, zero if high_block is None else roll(high_block, wide), high)
        return low + high

    def plane(p, near, member):
        def at(offset):
            return None if near[offset] is None else near[offset][member]

        across = sides(p, at((-1, 0)), at((1, 0)), low_x, high_x, cy, (cx - 1) * cy)
        along = sides(p, at((0, -1)), at((0, 1)), low_y, high_y, 1, cy - 1)
        return 4.0 * p - (across + along)

    def node_mirror(p):
        low = roll(p, 1, 0)
        inner = jnp.where(first_sub, jnp.where(first_group, p, roll(low, cells)), low)
        high = roll(p, -1, 0)
        outer = jnp.where(last_sub, jnp.where(last_group, p, roll(high, -cells)), high)
        return 2.0 * p - inner - outer

    def node_mean(value):
        total = jnp.broadcast_to(jnp.sum(value, axis=0, keepdims=True), (subs, LANES))
        parts = [total] + [roll(total, g * cells) for g in range(1, groups)]
        return add(parts) * (1.0 / nodes)

    nowhere = {(-1, 0): None, (1, 0): None, (0, -1): None, (0, 1): None}

    def pots_image(field, near, surface, fixed):
        p, v = field
        current = fixed[0] * (p - v)
        new_p = (
            node_cond * node_mirror(p)
            + current
            - fixed[1] * surface
            + plane_cond * plane(p, near, 0)
        )
        new_v = collector_cond * plane(v, near, 1) - node_mean(current)
        return new_p, new_v, current

    def relate(image, here, before, terms):
        alpha, gamma, _, inverse = terms
        value = image - alpha * here
        if gamma is not None:
            value = value - gamma * before
        return value * inverse

    def shell_images(levels, before, current, diffusion, terms):
        out = []
        for k in range(len(levels) - 1):
            here = levels[k]
            image = here + diffusion * (
                here - levels[k + 1] if k == 0 else 2.0 * here - levels[k - 1] - levels[k + 1]
            )
            if k == 0:
                image = image + current
            out.append(relate(image, here, before[k] if before else None, terms))
        return out

    def full_image(k, current, terms, fields, source=None, target=None):
        alpha, gamma, _, inverse = terms
        keep = (1.0 - alpha) * inverse
        spread = diff * inverse
        middle = (keep + 2.0 * spread)[None]
        spread = spread[None]
        basis[k, 0] = basis[k, 1]
        basis[k, shells + 1] = basis[k, shells]
        newest = fields[k + 1]
        starts = [
            fields[i][0] * newest[0] + fields[i][1] * (newest[1] * single) for i in range(k + 2)
        ]
        pushed = inverse * current

        def part(at, carry, last):
            here = basis[k, pl.ds(at + 1, CHUNK)]
            low = basis[k, pl.ds(at, CHUNK)]
            high = basis[k, pl.ds(at + 2, CHUNK)]
            new = middle * here - spread * (low + high)
            if gamma is not None:
                new = new - (gamma * inverse) * basis[k - 1, pl.ds(at + 1, CHUNK)]
            if last:
                new = jnp.concatenate([new[:-1], new[-1:] + pushed[None]], axis=0)
            basis[k + 1, pl.ds(at + 1, CHUNK)] = new
            others = [basis[i, pl.ds(at + 1, CHUNK)] for i in range(k)] + [here, new]
            return tuple(c + jnp.sum(o * new, axis=0) for c, o in zip(carry, others))

        parts = shells // CHUNK
        carry = lax.fori_loop(
            0, parts - 1, lambda c, carry: part(c * CHUNK, carry, False), tuple(starts)
        )
        return list(part((parts - 1) * CHUNK, carry, True))

    def line_up(products, offset):
        padded = -(-len(products) // 8) * 8
        stacked = [jnp.sum(d, axis=0, keepdims=True) for d in products]
        stacked += [zero[:1]] * (padded - len(products))
        tall = jnp.sum(jnp.concatenate(stacked, axis=0), axis=1, keepdims=True)
        at_row = lax.broadcasted_iota(jnp.int32, (padded, LANES), 0) + offset
        at_lane = lax.broadcasted_iota(jnp.int32, (padded, LANES), 1)
        return jnp.sum(jnp.where(at_row == at_lane, tall, 0.0), axis=0, keepdims=True)

    def row_copy(step, px, py):
        return pltpu.make_async_remote_copy(
            src_ref=sent_rows.at[step],
            dst_ref=rows.at[step, me],
            send_sem=row_send.at[step],
            recv_sem=row_recv.at[step],
            device_id={"gx": px, "gy": py},
            device_id_type=MESH,
        )

    def send_row(step, row):
        sent_rows[step] = row
        rows[step, me] = row
        peers(lambda px, py: row_copy(step, px, py).start())

    def take_row(step, wanted):
        part = rows.at[step, pl.ds(0, count - 1)]
        pltpu.make_async_copy(part, part, row_recv.at[step]).wait()
        total = jnp.sum(rows[step], axis=0)
        return [jnp.broadcast_to(total[:, k : k + 1], (subs, LANES)) for k in range(wanted)]

    def copies_of(phase):
        depth = PLAN[phase]
        out = []
        for o in order:
            if around[o] > depth:
                continue
            a, b = o
            items = 2 + depth - around[o]
            out.append(
                (
                    o,
                    pltpu.make_async_remote_copy(
                        src_ref=sent.at[phase, pl.ds(0, items)],
                        dst_ref=halos.at[phase, place[-a, -b], pl.ds(0, items)],
                        send_sem=edge_send.at[phase, place[o]],
                        recv_sem=edge_recv.at[phase, place[-a, -b]],
                        device_id={
                            "gx": lax.rem(mx + a + nx * deepest, nx),
                            "gy": lax.rem(my + b + ny * deepest, ny),
                        },
                        device_id_type=MESH,
                    ),
                )
            )
        return out

    def arrivals_of(phase):
        depth = PLAN[phase]
        out = []
        for o in order:
            if around[o] > depth:
                continue
            items = 2 + depth - around[o]
            part = halos.at[phase, place[o], pl.ds(0, items)]
            out.append((o, pltpu.make_async_copy(part, part, edge_recv.at[phase, place[o]])))
        return out

    def fixed_copies():
        out = []
        for o in order:
            if around[o] > deepest - 1:
                continue
            a, b = o
            items = 3 if around[o] <= deepest - 2 else 2
            part = fixed_halos.at[place[o], pl.ds(0, items)]
            out.append(
                (
                    o,
                    pltpu.make_async_remote_copy(
                        src_ref=fixed_sent.at[pl.ds(0, items)],
                        dst_ref=fixed_halos.at[place[-a, -b], pl.ds(0, items)],
                        send_sem=fixed_send.at[place[o]],
                        recv_sem=fixed_recv.at[place[-a, -b]],
                        device_id={
                            "gx": lax.rem(mx + a + nx * deepest, nx),
                            "gy": lax.rem(my + b + ny * deepest, ny),
                        },
                        device_id_type=MESH,
                    ),
                    pltpu.make_async_copy(part, part, fixed_recv.at[place[o]]),
                )
            )
        return out

    def send_edges(phase, field, levels):
        sent[phase, 0] = field[0]
        sent[phase, 1] = field[1]
        for k, level in enumerate(levels):
            sent[phase, 2 + k] = level
        for o, copy in copies_of(phase):
            pl.when(there[o])(copy.start)

    def tops(k, number):
        return [basis[k, shells - j] for j in range(number)]

    for copy in loads:
        copy.wait()
    turned_t = turned[...].T.reshape(subs, shells, LANES)
    for s in range(subs):
        basis[0, 1 : shells + 1, s, :] = turned_t[s]

    fields = [(pot, vol)] + [None] * ITERS
    fixed_own = (exch, slope)
    guess = [(center, None, radius, 1.0 / radius), (center, radius / 2, radius / 2, 2.0 / radius)]

    pl.semaphore_wait(barrier, count - 1)
    send_edges(0, fields[0], tops(0, PLAN[0] - 1))
    fixed_moves = fixed_copies()
    for o, copy, _ in fixed_moves:
        pl.when(there[o])(copy.start)

    local = [fields[0]]
    products = [
        pot * pot
        + vol * (vol * single)
        + lax.fori_loop(
            0,
            shells // CHUNK,
            lambda c, t: t
            + jnp.sum(
                basis[0, pl.ds(c * CHUNK + 1, CHUNK)] * basis[0, pl.ds(c * CHUNK + 1, CHUNK)],
                axis=0,
            ),
            zero,
        )
    ]
    first_square = products[0]
    for k in range(ADAPTIVE):
        new_p, new_v, current = pots_image(local[k], nowhere, basis[k, shells], fixed_own)
        before = local[k - 1] if k else (None, None)
        local.append(
            (
                relate(new_p, local[k][0], before[0], guess[k]),
                relate(new_v, local[k][1], before[1], guess[k]),
            )
        )
        products += full_image(k, current, guess[k], local)
    send_row(0, line_up(products, 0))

    def symmetric(sums, size):
        gram = [[None] * size for _ in range(size)]
        at = 0
        for j in range(size):
            for i in range(j + 1):
                gram[i][j] = gram[j][i] = sums[at]
                at += 1
        return gram

    def lanczos(sums):
        upper, inverse = factor(symmetric(sums, ADAPTIVE + 1))
        columns = project(upper, inverse, [(a, g, b) for a, g, b, _ in guess])
        out = []
        for k in range(ADAPTIVE):
            height = jnp.maximum(columns[k][k + 1], least_height)
            gamma = columns[k][k - 1] if k else None
            out.append((columns[k][k], gamma, height, 1.0 / height))
        return out

    recurrence = None
    row = line_up([first_square], 0)
    at = 1
    k = 0
    earlier = {}
    for phase, depth in enumerate(PLAN):
        more = phase + 1 < len(PLAN)
        ahead = PLAN[phase + 1] - 1 if more else 0
        if phase == 0:
            recurrence = lanczos(take_row(0, len(products)))
        for step in range(depth):
            if k + step < ADAPTIVE:
                continue
            gamma = radius / 2 if step or depth <= 2 else None
            recurrence.append((center, gamma, radius / 2, 2.0 / radius))
        for o, copy in arrivals_of(phase):
            pl.when(there[o])(copy.wait)
        if phase == 0:
            fixed = {(0, 0): (exch, slope, diff)}
            for o, _, wait in fixed_moves:
                pl.when(there[o])(wait.wait)
            for o, _, _ in fixed_moves:
                fixed[o] = tuple(
                    jnp.where(there[o], fixed_halos[place[o], i], 0.0)
                    for i in range(3 if around[o] <= deepest - 2 else 2)
                )
        now = {(0, 0): fields[k]}
        levels = {(0, 0): tops(k, depth + ahead)}
        before = {(0, 0): tops(k - 1, depth + ahead - 1) if k else None}
        for o in order:
            if around[o] <= depth:
                now[o] = tuple(
                    jnp.where(there[o], halos[phase, place[o], i], 0.0) for i in range(2)
                )
                levels[o] = [
                    jnp.where(there[o], halos[phase, place[o], 2 + i], 0.0)
                    for i in range(depth - around[o])
                ]
                before[o] = None
        currents = []
        past = earlier
        if k:
            past = dict(earlier)
            past[0, 0] = fields[k - 1]
        for step in range(depth):
            terms = recurrence[k + step]
            reach = depth - step - 1
            new, new_levels = {}, {}
            for o in now:
                if o != (0, 0) and around[o] > reach:
                    continue
                near = {
                    side: now.get((o[0] + side[0], o[1] + side[1])) for side in nowhere
                }
                new_p, new_v, current = pots_image(now[o], near, levels[o][0], fixed[o])
                last = past.get(o, (None, None))
                p = relate(new_p, now[o][0], last[0], terms)
                v = relate(new_v, now[o][1], last[1], terms)
                if o != (0, 0):
                    p = jnp.where(there[o], p, 0.0)
                    v = jnp.where(there[o], v, 0.0)
                else:
                    currents.append(current)
                new[o] = (p, v)
                if len(levels[o]) > 1:
                    new_levels[o] = shell_images(
                        levels[o], before[o], current, fixed[o][2], terms
                    )
                else:
                    new_levels[o] = []
            past, now = now, new
            before, levels = levels, new_levels
            fields[k + step + 1] = now[0, 0]
        earlier = {o: f for o, f in past.items() if o != (0, 0)}
        if more:
            send_edges(phase + 1, fields[k + depth], levels[0, 0])
        for step in range(depth):
            products = full_image(k + step, currents[step], recurrence[k + step], fields)
            row = row + line_up(products, at)
            at += len(products)
        k += depth
    send_row(1, row)
    gram = symmetric(take_row(1, at), ITERS + 1)
    upper, inverse = factor(gram)
    images = project(upper, inverse, [(a, g, b) for a, g, b, _ in recurrence])
    start, vectors, columns = arnoldi(upper, inverse, images, ITERS)
    weights = expand(least_squares(columns, start), vectors, upper, inverse)

    sol_p = add([w * f[0] for w, f in zip(weights, fields)])
    sol_v = add([w * f[1] for w, f in zip(weights, fields)])

    def gather(c, carry):
        at = c * CHUNK
        parts = [weights[i][None] * basis[i, pl.ds(at + 1, CHUNK)] for i in range(ITERS)]
        basis[ITERS, pl.ds(at + 1, CHUNK)] = add(parts)
        return carry

    lax.fori_loop(0, shells // CHUNK, gather, 0)
    flat = jnp.concatenate([basis[ITERS, 1 : shells + 1, s, :] for s in range(subs)], axis=0)
    turned[...] = flat.T
    stores = []
    for x in range(cx):
        for g in range(groups):
            edge_row = g * cells + x * cy
            stores.append(
                pltpu.make_async_copy(
                    turned.at[edge_row : edge_row + cy, :],
                    sol_conc_ref.at[x, :, g * span : (g + 1) * span],
                    out_sem.at[x, g],
                )
            )
    for copy in stores:
        copy.start()
    flat_p = jnp.concatenate(
        [sol_p[:, g * cells : (g + 1) * cells] for g in range(groups)] + [sol_v[:1, :cells]], axis=0
    )
    sol_pots_ref[...] = flat_p.T.reshape(cx, cy, nodes + 1)

    for phase in range(len(PLAN)):
        for o, copy in copies_of(phase):
            pl.when(there[o])(copy.wait_send)
    for o, copy, _ in fixed_moves:
        pl.when(there[o])(copy.wait_send)
    for step in range(2):
        part = rows.at[step, pl.ds(0, count - 1)]
        pltpu.make_async_copy(part, part, row_send.at[step]).wait()
    for copy in stores:
        copy.wait()


def solution(mesh):
    sizes = (mesh.shape["gx"], mesh.shape["gy"])
    count = sizes[0] * sizes[1]

    def shards(rhs_conc, rhs_pots, diffusion, exchange, slope):
        cx, cy = rhs_conc.shape[0], rhs_conc.shape[1]
        cells = cx * cy
        nodes = exchange.shape[2]
        shells = rhs_conc.shape[2] // nodes
        groups = LANES // cells
        subs = nodes // groups
        deepest = max(PLAN)
        near = len(surroundings(cx, cy, deepest))
        phases = len(PLAN)
        vmem = pl.BlockSpec(memory_space=pltpu.VMEM)
        anywhere = pl.BlockSpec(memory_space=pl.ANY)
        dma = pltpu.SemaphoreType.DMA
        return pl.pallas_call(
            functools.partial(cycle, sizes),
            out_shape=(
                jax.ShapeDtypeStruct(rhs_conc.shape, jnp.float32),
                jax.ShapeDtypeStruct(rhs_pots.shape, jnp.float32),
            ),
            in_specs=[anywhere] * 5,
            out_specs=(anywhere, vmem),
            scratch_shapes=[
                pltpu.VMEM((LANES, subs * shells), jnp.float32),
                pltpu.VMEM((ITERS + 1, shells + 2, subs, LANES), jnp.float32),
                pltpu.VMEM(rhs_pots.shape, jnp.float32),
                pltpu.VMEM((3,) + exchange.shape, jnp.float32),
                pltpu.VMEM((phases, deepest + 1, subs, LANES), jnp.float32),
                pltpu.VMEM((phases, near, deepest + 1, subs, LANES), jnp.float32),
                pltpu.VMEM((3, subs, LANES), jnp.float32),
                pltpu.VMEM((near, 3, subs, LANES), jnp.float32),
                pltpu.VMEM((2, count, 1, LANES), jnp.float32),
                pltpu.VMEM((2, 1, LANES), jnp.float32),
                dma((phases, near)),
                dma((phases, near)),
                dma((near,)),
                dma((near,)),
                dma((2,)),
                dma((2,)),
                dma((cx, groups)),
                dma((4,)),
                dma((cx, groups)),
            ],
            compiler_params=pltpu.CompilerParams(collective_id=0, has_side_effects=True),
        )(rhs_conc, rhs_pots, diffusion, exchange, slope)

    spec = P("gx", "gy", None)
    return jax.shard_map(
        shards,
        mesh=mesh,
        in_specs=(spec,) * 5,
        out_specs=(spec, spec),
        check_vma=False,
    )
```

time: 47.1 us -> 37.1 us (0.79)
  Pallas kernels: 43.8 us -> 34 us
    pallas_call x1, Pallas kernels: 43.8 us -> 34 us  [shards(): pl.pallas_call(functools.partial(cycle, sizes), out_shape=(jax.ShapeDtype...]
where the time goes in v1:
time: 37.1 us; the launch traced here: 36.9 us
  Pallas kernels  34 us (92%)
  local copies, waits for them, and re-layouts  2.28 us (6%)
  between operations  0.65 us (2%)
    pallas_call x1, Pallas kernels, shards(): pl.pallas_call(functools.partial(cycle, sizes), out_shape=(jax.ShapeDtype...  34 us
    unnamed x4, local copies, waits for them, and re-layouts  2.28 us

profile of v1, /device:TPU:0, one launch (start us, length us, event | category | flops | bytes accessed | tf_op | source)
XLA Modules:
  0.0 36.9 jit_solution(16329889312716058076)
XLA Ops:
  0.6 34.0 %shard_map.68 = (f32[2,16,2048]{2,1,0:T(8,128)}, f32[2,16,33]{2,1,0:T(8,128)}) custom-call(f32[2,16,2048]{2,1,0:T(8,128)} %conc_ref.1, f32[2,16,33]{2,1,0:T(8,128)} %pots_ref.1, f32[2,16,32]{2,1,0:T(8,128)} %diff_ref.1, f32[2,16,32]{2,1,0:T(8,128)} %exch_ref.1, f32[2,16,32]{2,1,0:T(8,128)} %slope_ref.1), custom_call_target="tpu_custom_call" | custom-call | tf_op jit(solution)/shard_map/pallas_call | solution.py:689
  34.6 0.0 copy-start
  34.6 1.7 %copy.9 = f32[2,16,2048]{2,1,0:T(8,128)} copy(f32[2,16,2048]{2,1,0:T(8,128)} %get-tuple-element.4) | data formatting | bytes 524288
  36.3 0.0 copy-done
  36.3 0.6 %copy.10 = f32[2,16,33]{2,1,0:T(8,128)} copy(f32[2,16,33]{2,1,0:T(8,128)S(1)} %copy-done) | data formatting | bytes 8448
Async XLA Ops:
  34.6 1.7 %copy-start = (f32[2,16,33]{2,1,0:T(8,128)S(1)}, f32[2,16,33]{2,1,0:T(8,128)}, u32[]{:S(2)}) copy-start(f32[2,16,33]{2,1,0:T(8,128)} %get-tuple-element.5) | copy-start | bytes 12676

commit v2 on v1

--- a/solution.py
+++ b/solution.py
@@ -10,7 +10,7 @@
 ITERS = 10
 LANES = 128
 CHUNK = 16
-PLAN = (2, 2, 2, 2, 2)
+PLAN = (3, 4, 3)
 ADAPTIVE = 2
 
 node_cond = 1.0
@@ -157,7 +157,7 @@
     diff_ref,
     exch_ref,
     slope_ref,
-    sol_conc_ref,
+    sol_turned_ref,
     sol_pots_ref,
     turned,
     basis,
@@ -177,7 +177,6 @@
     row_recv,
     load_sem,
     small_sem,
-    out_sem,
 ):
     nx, ny = sizes
     count = nx * ny
@@ -390,10 +389,13 @@
             device_id_type=MESH,
         )
 
+    def send_row_only(step):
+        peers(lambda px, py: row_copy(step, px, py).start())
+
     def send_row(step, row):
         sent_rows[step] = row
         rows[step, me] = row
-        peers(lambda px, py: row_copy(step, px, py).start())
+        send_row_only(step)
 
     def take_row(step, wanted):
         part = rows.at[step, pl.ds(0, count - 1)]
@@ -465,13 +467,16 @@
             )
         return out
 
+    def start_edges(phase):
+        for o, copy in copies_of(phase):
+            pl.when(there[o])(copy.start)
+
     def send_edges(phase, field, levels):
         sent[phase, 0] = field[0]
         sent[phase, 1] = field[1]
         for k, level in enumerate(levels):
             sent[phase, 2 + k] = level
-        for o, copy in copies_of(phase):
-            pl.when(there[o])(copy.start)
+        start_edges(phase)
 
     def tops(k, number):
         return [basis[k, shells - j] for j in range(number)]
@@ -485,12 +490,6 @@
     fields = [(pot, vol)] + [None] * ITERS
     fixed_own = (exch, slope)
     guess = [(center, None, radius, 1.0 / radius), (center, radius / 2, radius / 2, 2.0 / radius)]
-
-    pl.semaphore_wait(barrier, count - 1)
-    send_edges(0, fields[0], tops(0, PLAN[0] - 1))
-    fixed_moves = fixed_copies()
-    for o, copy, _ in fixed_moves:
-        pl.when(there[o])(copy.start)
 
     local = [fields[0]]
     products = [
@@ -518,7 +517,19 @@
             )
         )
         products += full_image(k, current, guess[k], local)
-    send_row(0, line_up(products, 0))
+    local_row = line_up(products, 0)
+    sent[0, 0] = pot
+    sent[0, 1] = vol
+    for i, level in enumerate(tops(0, PLAN[0] - 1)):
+        sent[0, 2 + i] = level
+    sent_rows[0] = local_row
+    rows[0, me] = local_row
+    pl.semaphore_wait(barrier, count - 1)
+    send_row_only(0)
+    start_edges(0)
+    fixed_moves = fixed_copies()
+    for o, copy, _ in fixed_moves:
+        pl.when(there[o])(copy.start)
 
     def symmetric(sums, size):
         gram = [[None] * size for _ in range(size)]
@@ -553,7 +564,8 @@
             if k + step < ADAPTIVE:
                 continue
             gamma = radius / 2 if step or depth <= 2 else None
-            recurrence.append((center, gamma, radius / 2, 2.0 / radius))
+            beta = radius if gamma is None else radius / 2
+            recurrence.append((center, gamma, beta, 1.0 / beta))
         for o, copy in arrivals_of(phase):
             pl.when(there[o])(copy.wait)
         if phase == 0:
@@ -638,20 +650,7 @@
 
     lax.fori_loop(0, shells // CHUNK, gather, 0)
     flat = jnp.concatenate([basis[ITERS, 1 : shells + 1, s, :] for s in range(subs)], axis=0)
-    turned[...] = flat.T
-    stores = []
-    for x in range(cx):
-        for g in range(groups):
-            edge_row = g * cells + x * cy
-            stores.append(
-                pltpu.make_async_copy(
-                    turned.at[edge_row : edge_row + cy, :],
-                    sol_conc_ref.at[x, :, g * span : (g + 1) * span],
-                    out_sem.at[x, g],
-                )
-            )
-    for copy in stores:
-        copy.start()
+    sol_turned_ref[...] = flat.T
     flat_p = jnp.concatenate(
         [sol_p[:, g * cells : (g + 1) * cells] for g in range(groups)] + [sol_v[:1, :cells]], axis=0
     )
@@ -665,7 +664,27 @@
     for step in range(2):
         part = rows.at[step, pl.ds(0, count - 1)]
         pltpu.make_async_copy(part, part, row_send.at[step]).wait()
-    for copy in stores:
+
+
+def place_outputs(flat_ref, pots_ref, sol_conc_ref, sol_pots_ref, conc_sem, pots_sem):
+    cx, cy = sol_conc_ref.shape[0], sol_conc_ref.shape[1]
+    cells = cx * cy
+    groups = LANES // cells
+    span = flat_ref.shape[1]
+    copies = [pltpu.make_async_copy(pots_ref, sol_pots_ref, pots_sem)]
+    for x in range(cx):
+        for g in range(groups):
+            edge_row = g * cells + x * cy
+            copies.append(
+                pltpu.make_async_copy(
+                    flat_ref.at[edge_row : edge_row + cy, :],
+                    sol_conc_ref.at[x, :, g * span : (g + 1) * span],
+                    conc_sem.at[x, g],
+                )
+            )
+    for copy in copies:
+        copy.start()
+    for copy in copies:
         copy.wait()
 
 
@@ -686,14 +705,18 @@
         vmem = pl.BlockSpec(memory_space=pltpu.VMEM)
         anywhere = pl.BlockSpec(memory_space=pl.ANY)
         dma = pltpu.SemaphoreType.DMA
-        return pl.pallas_call(
+        inputs = [
+            pltpu.with_memory_space_constraint(x, pltpu.HBM)
+            for x in (rhs_conc, rhs_pots, diffusion, exchange, slope)
+        ]
+        flat, sol_pots = pl.pallas_call(
             functools.partial(cycle, sizes),
             out_shape=(
-                jax.ShapeDtypeStruct(rhs_conc.shape, jnp.float32),
+                jax.ShapeDtypeStruct((LANES, subs * shells), jnp.float32),
                 jax.ShapeDtypeStruct(rhs_pots.shape, jnp.float32),
             ),
             in_specs=[anywhere] * 5,
-            out_specs=(anywhere, vmem),
+            out_specs=(vmem, vmem),
             scratch_shapes=[
                 pltpu.VMEM((LANES, subs * shells), jnp.float32),
                 pltpu.VMEM((ITERS + 1, shells + 2, subs, LANES), jnp.float32),
@@ -713,10 +736,24 @@
                 dma((2,)),
                 dma((cx, groups)),
                 dma((4,)),
-                dma((cx, groups)),
             ],
-            compiler_params=pltpu.CompilerParams(collective_id=0, has_side_effects=True),
-        )(rhs_conc, rhs_pots, diffusion, exchange, slope)
+            compiler_params=pltpu.CompilerParams(
+                collective_id=0,
+                has_side_effects=True,
+                vmem_limit_bytes=12 * 1024 * 1024,
+            ),
+        )(*inputs)
+        return pl.pallas_call(
+            place_outputs,
+            out_shape=(
+                jax.ShapeDtypeStruct(rhs_conc.shape, jnp.float32),
+                jax.ShapeDtypeStruct(rhs_pots.shape, jnp.float32),
+            ),
+            in_specs=[vmem, vmem],
+            out_specs=(anywhere, anywhere),
+            scratch_shapes=[dma((cx, groups)), dma],
+            compiler_params=pltpu.CompilerParams(vmem_limit_bytes=12 * 1024 * 1024),
+        )(flat, sol_pots)
 
     spec = P("gx", "gy", None)
     return jax.shard_map(

time: 37.1 us -> 29.1 us (0.78)
  Pallas kernels: 34 us -> 28.2 us
  local copies, waits for them, and re-layouts: 2.28 us -> 0 us
    pallas_call x1, Pallas kernels: 34 us -> 27.5 us  [shards(): pl.pallas_call(functools.partial(cycle, sizes), out_shape=(jax.ShapeDtype...]
    unnamed x4 -> x0, local copies, waits for them, and re-layouts: 2.28 us -> none
    pallas_call x0 -> x1, Pallas kernels: none -> 0.78 us  [shards(): pl.pallas_call(place_outputs, out_shape=(jax.ShapeDtypeStruct(rhs_conc.sh...]
where the time goes in v2:
time: 29.1 us; the launch traced here: 28.9 us
  Pallas kernels  28.2 us (97%)
  between operations  0.64 us (2%)
    pallas_call x1, Pallas kernels, shards(): pl.pallas_call(functools.partial(cycle, sizes), out_shape=(jax.ShapeDtype...  27.5 us
    pallas_call x1, Pallas kernels, shards(): pl.pallas_call(place_outputs, out_shape=(jax.ShapeDtypeStruct(rhs_conc.sh...  0.78 us

profile of v2, /device:TPU:0, one launch (start us, length us, event | category | flops | bytes accessed | tf_op | source)
XLA Modules:
  0.0 28.9 jit_solution(17867826564995800295)
XLA Ops:
  0.6 27.5 %shard_map.68 = (f32[128,512]{1,0:T(8,128)S(1)}, f32[2,16,33]{2,1,0:T(8,128)S(1)}) custom-call(f32[2,16,2048]{2,1,0:T(8,128)} %conc_ref.1, f32[2,16,33]{2,1,0:T(8,128)} %pots_ref.1, f32[2,16,32]{2,1,0:T(8,128)} %diff_ref.1, f32[2,16,32]{2,1,0:T(8,128)} %exch_ref.1, f32[2,16,32]{2,1,0:T(8,128)} %slope_ref.1), custom_call_target="tpu_custom_call" | custom-call | tf_op jit(solution)/shard_map/pallas_call | solution.py:712
  28.1 0.8 %shard_map.69 = (f32[2,16,2048]{2,1,0:T(8,128)}, f32[2,16,33]{2,1,0:T(8,128)}) custom-call(f32[128,512]{1,0:T(8,128)S(1)} %get-tuple-element.4.flat_ref, f32[2,16,33]{2,1,0:T(8,128)S(1)} %get-tuple-element.5.pots_ref), custom_call_target="tpu_custom_call" | custom-call | tf_op jit(solution)/shard_map/pallas_call | solution.py:746

commit v3 on v2

--- a/solution.py
+++ b/solution.py
@@ -10,7 +10,7 @@
 ITERS = 10
 LANES = 128
 CHUNK = 16
-PLAN = (3, 4, 3)
+PLAN = (5, 5)
 ADAPTIVE = 2
 
 node_cond = 1.0
@@ -150,6 +150,24 @@
     return found
 
 
+def strip_slots(widths, room):
+    out, page, at = [], 0, 0
+    for width in widths:
+        if at + width > room:
+            page, at = page + 1, 0
+        out.append((page, at, width))
+        at += width
+    return out
+
+
+def phase_widths(depth):
+    return [depth, depth] + list(range(depth - 1, 0, -1))
+
+
+def pages_of(slots, number):
+    return 1 + max(page for page, _, _ in slots[:number])
+
+
 def cycle(
     sizes,
     conc_ref,
@@ -164,8 +182,10 @@
     raw_pots,
     raw_fixed,
     sent,
+    strips,
     halos,
     fixed_sent,
+    fixed_strips,
     fixed_halos,
     rows,
     sent_rows,
@@ -251,8 +271,6 @@
     pot = node_register(pots_t)
     vol_row = pots_t[nodes : nodes + 1, :]
     vol = jnp.broadcast_to(jnp.concatenate([vol_row] * groups, axis=1), (subs, LANES))
-    for k, value in enumerate((exch, slope, diff)):
-        fixed_sent[k] = value
 
     lane = lax.broadcasted_iota(jnp.int32, (subs, LANES), 1)
     sub = lax.broadcasted_iota(jnp.int32, (subs, LANES), 0)
@@ -276,6 +294,37 @@
     def roll(value, shift, axis=1):
         shift = shift % value.shape[axis]
         return pltpu.roll(value, shift, axis) if shift else value
+
+    def pack(values, slots, to_low):
+        packed = [zero] * pages_of(slots, len(slots))
+        for value, (page, at, width) in zip(values, slots):
+            if to_low:
+                held = (cell_y >= at) & (cell_y < at + width)
+                packed[page] = jnp.where(held, roll(value, at), packed[page])
+            else:
+                held = (cell_y >= cy - at - width) & (cell_y < cy - at)
+                packed[page] = jnp.where(held, roll(value, -at), packed[page])
+        return packed
+
+    def unpack(pages, slot, from_high):
+        page, at, width = slot
+        packed = pages[page]
+        if from_high:
+            return jnp.where(cell_y < width, roll(packed, -at), zero)
+        return jnp.where(cell_y >= cy - width, roll(packed, at), zero)
+
+    def phase_slots(phase):
+        return strip_slots(phase_widths(PLAN[phase]), cy)
+
+    fixed_slots = strip_slots([deepest - 1, deepest - 1, max(deepest - 2, 0)], cy)
+
+    def items_of(phase, o):
+        number = 2 + PLAN[phase] - around[o]
+        return pages_of(phase_slots(phase), number) if o[1] else number
+
+    def fixed_items_of(o):
+        number = 3 if around[o] <= deepest - 2 else 2
+        return pages_of(fixed_slots, number) if o[1] else number
 
     def sides(p, low_block, high_block, edge_low, edge_high, step, wide):
         low = roll(p, step)
@@ -410,12 +459,14 @@
             if around[o] > depth:
                 continue
             a, b = o
-            items = 2 + depth - around[o]
+            items = items_of(phase, o)
             out.append(
                 (
                     o,
                     pltpu.make_async_remote_copy(
-                        src_ref=sent.at[phase, pl.ds(0, items)],
+                        src_ref=strips.at[phase, (b + 1) // 2, pl.ds(0, items)]
+                        if b
+                        else sent.at[phase, pl.ds(0, items)],
                         dst_ref=halos.at[phase, place[-a, -b], pl.ds(0, items)],
                         send_sem=edge_send.at[phase, place[o]],
                         recv_sem=edge_recv.at[phase, place[-a, -b]],
@@ -435,7 +486,7 @@
         for o in order:
             if around[o] > depth:
                 continue
-            items = 2 + depth - around[o]
+            items = items_of(phase, o)
             part = halos.at[phase, place[o], pl.ds(0, items)]
             out.append((o, pltpu.make_async_copy(part, part, edge_recv.at[phase, place[o]])))
         return out
@@ -446,13 +497,15 @@
             if around[o] > deepest - 1:
                 continue
             a, b = o
-            items = 3 if around[o] <= deepest - 2 else 2
+            items = fixed_items_of(o)
             part = fixed_halos.at[place[o], pl.ds(0, items)]
             out.append(
                 (
                     o,
                     pltpu.make_async_remote_copy(
-                        src_ref=fixed_sent.at[pl.ds(0, items)],
+                        src_ref=fixed_strips.at[(b + 1) // 2, pl.ds(0, items)]
+                        if b
+                        else fixed_sent.at[pl.ds(0, items)],
                         dst_ref=fixed_halos.at[place[-a, -b], pl.ds(0, items)],
                         send_sem=fixed_send.at[place[o]],
                         recv_sem=fixed_recv.at[place[-a, -b]],
@@ -471,11 +524,16 @@
         for o, copy in copies_of(phase):
             pl.when(there[o])(copy.start)
 
+    def store_edges(phase, field, levels):
+        values = [field[0], field[1]] + list(levels)
+        for k, value in enumerate(values):
+            sent[phase, k] = value
+        for k in range(2):
+            for page, packed in enumerate(pack(values, phase_slots(phase), k == 0)):
+                strips[phase, k, page] = packed
+
     def send_edges(phase, field, levels):
-        sent[phase, 0] = field[0]
-        sent[phase, 1] = field[1]
-        for k, level in enumerate(levels):
-            sent[phase, 2 + k] = level
+        store_edges(phase, field, levels)
         start_edges(phase)
 
     def tops(k, number):
@@ -518,10 +576,12 @@
         )
         products += full_image(k, current, guess[k], local)
     local_row = line_up(products, 0)
-    sent[0, 0] = pot
-    sent[0, 1] = vol
-    for i, level in enumerate(tops(0, PLAN[0] - 1)):
-        sent[0, 2 + i] = level
+    store_edges(0, fields[0], tops(0, PLAN[0] - 1))
+    for k, value in enumerate((exch, slope, diff)):
+        fixed_sent[k] = value
+    for k in range(2):
+        for page, packed in enumerate(pack((exch, slope, diff), fixed_slots, k == 0)):
+            fixed_strips[k, page] = packed
     sent_rows[0] = local_row
     rows[0, me] = local_row
     pl.semaphore_wait(barrier, count - 1)
@@ -573,22 +633,29 @@
             for o, _, wait in fixed_moves:
                 pl.when(there[o])(wait.wait)
             for o, _, _ in fixed_moves:
-                fixed[o] = tuple(
+                number = 3 if around[o] <= deepest - 2 else 2
+                got = [
                     jnp.where(there[o], fixed_halos[place[o], i], 0.0)
-                    for i in range(3 if around[o] <= deepest - 2 else 2)
-                )
+                    for i in range(fixed_items_of(o))
+                ]
+                if o[1]:
+                    got = [unpack(got, fixed_slots[i], o[1] > 0) for i in range(number)]
+                fixed[o] = tuple(got)
         now = {(0, 0): fields[k]}
         levels = {(0, 0): tops(k, depth + ahead)}
         before = {(0, 0): tops(k - 1, depth + ahead - 1) if k else None}
         for o in order:
             if around[o] <= depth:
-                now[o] = tuple(
-                    jnp.where(there[o], halos[phase, place[o], i], 0.0) for i in range(2)
-                )
-                levels[o] = [
-                    jnp.where(there[o], halos[phase, place[o], 2 + i], 0.0)
-                    for i in range(depth - around[o])
+                number = 2 + depth - around[o]
+                got = [
+                    jnp.where(there[o], halos[phase, place[o], i], 0.0)
+                    for i in range(items_of(phase, o))
                 ]
+                if o[1]:
+                    slots = phase_slots(phase)
+                    got = [unpack(got, slots[i], o[1] > 0) for i in range(number)]
+                now[o] = tuple(got[:2])
+                levels[o] = got[2:]
                 before[o] = None
         currents = []
         past = earlier
@@ -702,6 +769,8 @@
         deepest = max(PLAN)
         near = len(surroundings(cx, cy, deepest))
         phases = len(PLAN)
+        widest = strip_slots(phase_widths(deepest), cy)
+        pages = pages_of(widest, len(widest))
         vmem = pl.BlockSpec(memory_space=pltpu.VMEM)
         anywhere = pl.BlockSpec(memory_space=pl.ANY)
         dma = pltpu.SemaphoreType.DMA
@@ -723,8 +792,10 @@
                 pltpu.VMEM(rhs_pots.shape, jnp.float32),
                 pltpu.VMEM((3,) + exchange.shape, jnp.float32),
                 pltpu.VMEM((phases, deepest + 1, subs, LANES), jnp.float32),
+                pltpu.VMEM((phases, 2, pages, subs, LANES), jnp.float32),
                 pltpu.VMEM((phases, near, deepest + 1, subs, LANES), jnp.float32),
                 pltpu.VMEM((3, subs, LANES), jnp.float32),
+                pltpu.VMEM((2, pages, subs, LANES), jnp.float32),
                 pltpu.VMEM((near, 3, subs, LANES), jnp.float32),
                 pltpu.VMEM((2, count, 1, LANES), jnp.float32),
                 pltpu.VMEM((2, 1, LANES), jnp.float32),

time: 29.1 us -> 27.1 us (0.931)
  Pallas kernels: 28.2 us -> 26.2 us
    pallas_call x1, Pallas kernels: 27.5 us -> 25.5 us  [shards(): pl.pallas_call(functools.partial(cycle, sizes), out_shape=(jax.ShapeDtype...]
where the time goes in v3:
time: 27.1 us; the launch traced here: 26.9 us
  Pallas kernels  26.2 us (97%)
  between operations  0.64 us (2%)
    pallas_call x1, Pallas kernels, shards(): pl.pallas_call(functools.partial(cycle, sizes), out_shape=(jax.ShapeDtype...  25.5 us
    pallas_call x1, Pallas kernels, shards(): pl.pallas_call(place_outputs, out_shape=(jax.ShapeDtypeStruct(rhs_conc.sh...  0.78 us

profile of v3, /device:TPU:0, one launch (start us, length us, event | category | flops | bytes accessed | tf_op | source)
XLA Modules:
  0.0 26.9 jit_solution(15286537074805407680)
XLA Ops:
  0.6 25.5 %shard_map.68 = (f32[128,512]{1,0:T(8,128)S(1)}, f32[2,16,33]{2,1,0:T(8,128)S(1)}) custom-call(f32[2,16,2048]{2,1,0:T(8,128)} %conc_ref.1, f32[2,16,33]{2,1,0:T(8,128)} %pots_ref.1, f32[2,16,32]{2,1,0:T(8,128)} %diff_ref.1, f32[2,16,32]{2,1,0:T(8,128)} %exch_ref.1, f32[2,16,32]{2,1,0:T(8,128)} %slope_ref.1), custom_call_target="tpu_custom_call" | custom-call | tf_op jit(solution)/shard_map/pallas_call | solution.py:781
  26.1 0.8 %shard_map.69 = (f32[2,16,2048]{2,1,0:T(8,128)}, f32[2,16,33]{2,1,0:T(8,128)}) custom-call(f32[128,512]{1,0:T(8,128)S(1)} %get-tuple-element.4.flat_ref, f32[2,16,33]{2,1,0:T(8,128)S(1)} %get-tuple-element.5.pots_ref), custom_call_target="tpu_custom_call" | custom-call | tf_op jit(solution)/shard_map/pallas_call | solution.py:817

commit v4 on v3

--- a/solution.py
+++ b/solution.py
@@ -32,94 +32,86 @@
     return terms[0]
 
 
-def factor(gram):
-    size = len(gram)
-    left = [[gram[i][j] for j in range(size)] for i in range(size)]
-    upper = [[None] * size for _ in range(size)]
-    inverse = []
-    for k in range(size):
-        pivot = left[k][k]
-        good = pivot > least_pivot * gram[k][k]
-        inv = jnp.where(good, lax.rsqrt(jnp.where(good, pivot, 1.0)), 0.0)
-        inverse.append(inv)
-        upper[k][k] = pivot * inv
-        for j in range(k + 1, size):
-            upper[k][j] = left[k][j] * inv
-        for i in range(k + 1, size):
-            for j in range(i, size):
-                left[i][j] = left[i][j] - upper[k][i] * upper[k][j]
-    return upper, inverse
-
-
-def project(upper, inverse, recurrence):
-    columns = []
-    for k, (alpha, gamma, beta) in enumerate(recurrence):
-        column = []
-        for i in range(k + 2):
-            terms = [beta * upper[i][k + 1]]
-            if i <= k:
-                terms.append(alpha * upper[i][k])
-            if i <= k - 1 and gamma is not None:
-                terms.append(gamma * upper[i][k - 1])
-            value = add(terms)
-            known = [columns[m][i] * upper[m][k] for m in range(max(i - 1, 0), k)]
-            if known:
-                value = value - add(known)
-            column.append(value * inverse[k])
-        columns.append(column)
-    return columns
-
-
-def arnoldi(upper, inverse, images, count):
-    height = jnp.sqrt(upper[0][0] * upper[0][0] + epsilon)
-    start = height
-    vectors = [[upper[0][0] / height]]
-    columns = []
-    for j in range(count):
-        newest = vectors[j]
-        image = [
-            add([images[k][t] * newest[k] for k in range(max(t - 1, 0), j + 1)])
-            for t in range(j + 2)
-        ]
-        coeffs = [
-            add([vectors[i][t] * image[t] for t in range(i + 1)]) for i in range(j + 1)
-        ]
-        rest = [
-            image[t] - add([coeffs[i] * vectors[i][t] for i in range(t, j + 1)])
-            for t in range(j + 1)
-        ] + [image[j + 1]]
-        height = jnp.sqrt(add([r * r for r in rest]) + epsilon)
-        columns.append(coeffs + [height])
-        if j + 1 < count:
-            scale = 1.0 / height
-            vectors.append([r * scale for r in rest])
-    return start, vectors, columns
-
-
-def least_squares(columns, start):
-    target, cosines, sines, uppers = [start], [], [], []
-    for step, column in enumerate(columns):
-        entries = list(column)
-        for row in range(step):
-            first = cosines[row] * entries[row] + sines[row] * entries[row + 1]
-            second = cosines[row] * entries[row + 1] - sines[row] * entries[row]
-            entries[row] = first
-            entries[row + 1] = second
-        size = jnp.sqrt(entries[step] * entries[step] + entries[step + 1] * entries[step + 1])
-        shrink = 1.0 / size
-        cosine = entries[step] * shrink
-        sine = entries[step + 1] * shrink
-        entries[step] = size
-        cosines.append(cosine)
-        sines.append(sine)
-        lead = target[step]
-        target[step] = cosine * lead
-        target.append(-sine * lead)
-        uppers.append((entries[: step + 1], shrink))
-    weights = [None] * len(columns)
-    for row in range(len(columns) - 1, -1, -1):
+def factor_column(gram, upper, inverse):
+    j = len(inverse)
+    column = []
+    for i in range(j):
+        value = gram[i][j]
+        if i:
+            value = value - add([upper[i][m] * column[m] for m in range(i)])
+        column.append(value * inverse[i])
+    pivot = gram[j][j]
+    if j:
+        pivot = pivot - add([c * c for c in column])
+    good = pivot > least_pivot * gram[j][j]
+    inv = jnp.where(good, lax.rsqrt(jnp.where(good, pivot, 1.0)), 0.0)
+    upper.append(column + [pivot * inv])
+    inverse.append(inv)
+
+
+def project_column(upper, inverse, recurrence, columns):
+    k = len(columns)
+    alpha, gamma, beta = recurrence[k]
+    column = []
+    for i in range(k + 2):
+        terms = [beta * upper[k + 1][i]]
+        if i <= k:
+            terms.append(alpha * upper[k][i])
+        if i <= k - 1 and gamma is not None:
+            terms.append(gamma * upper[k - 1][i])
+        value = add(terms)
+        known = [columns[m][i] * upper[k][m] for m in range(max(i - 1, 0), k)]
+        if known:
+            value = value - add(known)
+        column.append(value * inverse[k])
+    columns.append(column)
+
+
+def arnoldi_column(images, vectors):
+    j = len(vectors) - 1
+    newest = vectors[j]
+    image = [
+        add([images[k][t] * newest[k] for k in range(max(t - 1, 0), j + 1)]) for t in range(j + 2)
+    ]
+    coeffs = [add([vectors[i][t] * image[t] for t in range(i + 1)]) for i in range(j + 1)]
+    rest = [
+        image[t] - add([coeffs[i] * vectors[i][t] for i in range(t, j + 1)]) for t in range(j + 1)
+    ] + [image[j + 1]]
+    square = add([r * r for r in rest]) + epsilon
+    scale = lax.rsqrt(square)
+    height = square * scale
+    vectors.append([r * scale for r in rest])
+    return coeffs + [height]
+
+
+def rotate_column(entries, target, cosines, sines, uppers):
+    step = len(uppers)
+    entries = list(entries)
+    for row in range(step):
+        first = cosines[row] * entries[row] + sines[row] * entries[row + 1]
+        second = cosines[row] * entries[row + 1] - sines[row] * entries[row]
+        entries[row] = first
+        entries[row + 1] = second
+    square = entries[step] * entries[step] + entries[step + 1] * entries[step + 1]
+    shrink = lax.rsqrt(square)
+    size = square * shrink
+    cosine = entries[step] * shrink
+    sine = entries[step + 1] * shrink
+    entries[step] = size
+    cosines.append(cosine)
+    sines.append(sine)
+    lead = target[step]
+    target[step] = cosine * lead
+    target.append(-sine * lead)
+    uppers.append((entries[: step + 1], shrink))
+
+
+def back_substitute(target, uppers):
+    count = len(uppers)
+    weights = [None] * count
+    for row in range(count - 1, -1, -1):
         total = target[row]
-        for later in range(len(columns) - 1, row, -1):
+        for later in range(count - 1, row, -1):
             total = total - uppers[later][0][row] * weights[later]
         weights[row] = total * uppers[row][1]
     return weights
@@ -132,7 +124,7 @@
     for row in range(count - 1, -1, -1):
         total = along[row]
         for later in range(count - 1, row, -1):
-            total = total - upper[row][later] * out[later]
+            total = total - upper[later][row] * out[later]
         out[row] = total * inverse[row]
     return out
 
@@ -184,15 +176,10 @@
     sent,
     strips,
     halos,
-    fixed_sent,
-    fixed_strips,
-    fixed_halos,
     rows,
     sent_rows,
     edge_send,
     edge_recv,
-    fixed_send,
-    fixed_recv,
     row_send,
     row_recv,
     load_sem,
@@ -284,6 +271,7 @@
     low_x, high_x = cell_x == 0, cell_x == cx - 1
     low_y, high_y = cell_y == 0, cell_y == cy - 1
     zero = jnp.zeros((subs, LANES), jnp.float32)
+    middle = (subs - 1) // 2
 
     there = {}
     for a, b in order:
@@ -322,9 +310,15 @@
         number = 2 + PLAN[phase] - around[o]
         return pages_of(phase_slots(phase), number) if o[1] else number
 
-    def fixed_items_of(o):
-        number = 3 if around[o] <= deepest - 2 else 2
-        return pages_of(fixed_slots, number) if o[1] else number
+    def first_of(phase, o):
+        if phase:
+            return 0
+        if o[1]:
+            return 0 if around[o] < deepest else 1
+        return {0: 3, 1: 1}.get(deepest - around[o], 0)
+
+    def offset_of(phase, b):
+        return 0 if phase else 1 if b else 3
 
     def sides(p, low_block, high_block, edge_low, edge_high, step, wide):
         low = roll(p, step)
@@ -386,36 +380,50 @@
             out.append(relate(image, here, before[k] if before else None, terms))
         return out
 
-    def full_image(k, current, terms, fields, source=None, target=None):
+    def pots_products(k, fields):
+        newest = fields[k + 1]
+        return [
+            fields[i][0] * newest[0] + fields[i][1] * (newest[1] * single) for i in range(k + 2)
+        ]
+
+    def image_shells(k, current, terms, straight=False):
         alpha, gamma, _, inverse = terms
         keep = (1.0 - alpha) * inverse
         spread = diff * inverse
-        middle = (keep + 2.0 * spread)[None]
+        middle_part = (keep + 2.0 * spread)[None]
         spread = spread[None]
         basis[k, 0] = basis[k, 1]
         basis[k, shells + 1] = basis[k, shells]
-        newest = fields[k + 1]
-        starts = [
-            fields[i][0] * newest[0] + fields[i][1] * (newest[1] * single) for i in range(k + 2)
-        ]
         pushed = inverse * current
+        drag = None if gamma is None else gamma * inverse
 
         def part(at, carry, last):
             here = basis[k, pl.ds(at + 1, CHUNK)]
             low = basis[k, pl.ds(at, CHUNK)]
             high = basis[k, pl.ds(at + 2, CHUNK)]
-            new = middle * here - spread * (low + high)
-            if gamma is not None:
-                new = new - (gamma * inverse) * basis[k - 1, pl.ds(at + 1, CHUNK)]
+            new = middle_part * here - spread * (low + high)
+            others = [basis[i, pl.ds(at + 1, CHUNK)] for i in range(k)] + [here]
+            if drag is not None:
+                behind = others[k - 1]
+                new = new - (behind if isinstance(drag, float) and drag == 1.0 else drag * behind)
             if last:
                 new = jnp.concatenate([new[:-1], new[-1:] + pushed[None]], axis=0)
             basis[k + 1, pl.ds(at + 1, CHUNK)] = new
-            others = [basis[i, pl.ds(at + 1, CHUNK)] for i in range(k)] + [here, new]
-            return tuple(c + jnp.sum(o * new, axis=0) for c, o in zip(carry, others))
+            return tuple(
+                c + jnp.sum(o * new, axis=0) for c, o in zip(carry, others + [new])
+            )
 
         parts = shells // CHUNK
+        if straight:
+            carry = (zero,) * (k + 2)
+            for c in range(parts - 1):
+                carry = part(c * CHUNK, carry, False)
+            return list(part((parts - 1) * CHUNK, carry, True))
         carry = lax.fori_loop(
-            0, parts - 1, lambda c, carry: part(c * CHUNK, carry, False), tuple(starts)
+            0,
+            parts - 1,
+            lambda c, carry: part(c * CHUNK, carry, False),
+            (zero,) * (k + 2),
         )
         return list(part((parts - 1) * CHUNK, carry, True))
 
@@ -459,15 +467,16 @@
             if around[o] > depth:
                 continue
             a, b = o
-            items = items_of(phase, o)
+            start = first_of(phase, o)
+            items = offset_of(phase, b) + items_of(phase, o) - start
             out.append(
                 (
                     o,
                     pltpu.make_async_remote_copy(
-                        src_ref=strips.at[phase, (b + 1) // 2, pl.ds(0, items)]
+                        src_ref=strips.at[phase, (b + 1) // 2, pl.ds(start, items)]
                         if b
-                        else sent.at[phase, pl.ds(0, items)],
-                        dst_ref=halos.at[phase, place[-a, -b], pl.ds(0, items)],
+                        else sent.at[phase, pl.ds(start, items)],
+                        dst_ref=halos.at[phase, place[-a, -b], pl.ds(start, items)],
                         send_sem=edge_send.at[phase, place[o]],
                         recv_sem=edge_recv.at[phase, place[-a, -b]],
                         device_id={
@@ -486,38 +495,10 @@
         for o in order:
             if around[o] > depth:
                 continue
-            items = items_of(phase, o)
-            part = halos.at[phase, place[o], pl.ds(0, items)]
+            start = first_of(phase, o)
+            items = offset_of(phase, o[1]) + items_of(phase, o) - start
+            part = halos.at[phase, place[o], pl.ds(start, items)]
             out.append((o, pltpu.make_async_copy(part, part, edge_recv.at[phase, place[o]])))
-        return out
-
-    def fixed_copies():
-        out = []
-        for o in order:
-            if around[o] > deepest - 1:
-                continue
-            a, b = o
-            items = fixed_items_of(o)
-            part = fixed_halos.at[place[o], pl.ds(0, items)]
-            out.append(
-                (
-                    o,
-                    pltpu.make_async_remote_copy(
-                        src_ref=fixed_strips.at[(b + 1) // 2, pl.ds(0, items)]
-                        if b
-                        else fixed_sent.at[pl.ds(0, items)],
-                        dst_ref=fixed_halos.at[place[-a, -b], pl.ds(0, items)],
-                        send_sem=fixed_send.at[place[o]],
-                        recv_sem=fixed_recv.at[place[-a, -b]],
-                        device_id={
-                            "gx": lax.rem(mx + a + nx * deepest, nx),
-                            "gy": lax.rem(my + b + ny * deepest, ny),
-                        },
-                        device_id_type=MESH,
-                    ),
-                    pltpu.make_async_copy(part, part, fixed_recv.at[place[o]]),
-                )
-            )
         return out
 
     def start_edges(phase):
@@ -527,10 +508,10 @@
     def store_edges(phase, field, levels):
         values = [field[0], field[1]] + list(levels)
         for k, value in enumerate(values):
-            sent[phase, k] = value
+            sent[phase, offset_of(phase, 0) + k] = value
         for k in range(2):
             for page, packed in enumerate(pack(values, phase_slots(phase), k == 0)):
-                strips[phase, k, page] = packed
+                strips[phase, k, offset_of(phase, 1) + page] = packed
 
     def send_edges(phase, field, levels):
         store_edges(phase, field, levels)
@@ -574,22 +555,20 @@
                 relate(new_v, local[k][1], before[1], guess[k]),
             )
         )
-        products += full_image(k, current, guess[k], local)
+        inner = image_shells(k, current, guess[k])
+        products += [c + o for c, o in zip(inner, pots_products(k, local))]
     local_row = line_up(products, 0)
+    local_count = len(products)
     store_edges(0, fields[0], tops(0, PLAN[0] - 1))
-    for k, value in enumerate((exch, slope, diff)):
-        fixed_sent[k] = value
+    for k, value in enumerate((diff, exch, slope)):
+        sent[0, k] = value
     for k in range(2):
-        for page, packed in enumerate(pack((exch, slope, diff), fixed_slots, k == 0)):
-            fixed_strips[k, page] = packed
+        strips[0, k, 0] = pack((exch, slope, diff), fixed_slots, k == 0)[0]
     sent_rows[0] = local_row
     rows[0, me] = local_row
     pl.semaphore_wait(barrier, count - 1)
+    start_edges(0)
     send_row_only(0)
-    start_edges(0)
-    fixed_moves = fixed_copies()
-    for o, copy, _ in fixed_moves:
-        pl.when(there[o])(copy.start)
 
     def symmetric(sums, size):
         gram = [[None] * size for _ in range(size)]
@@ -601,8 +580,12 @@
         return gram
 
     def lanczos(sums):
-        upper, inverse = factor(symmetric(sums, ADAPTIVE + 1))
-        columns = project(upper, inverse, [(a, g, b) for a, g, b, _ in guess])
+        gram = symmetric(sums, ADAPTIVE + 1)
+        upper, inverse, columns = [], [], []
+        for k in range(ADAPTIVE + 1):
+            factor_column(gram, upper, inverse)
+            if k:
+                project_column(upper, inverse, [g[:3] for g in guess], columns)
         out = []
         for k in range(ADAPTIVE):
             height = jnp.maximum(columns[k][k + 1], least_height)
@@ -611,112 +594,208 @@
         return out
 
     recurrence = None
-    row = line_up([first_square], 0)
-    at = 1
+    restart = (center, None, radius, 1.0 / radius)
+    usual = (center, radius / 2, radius / 2, 2.0 / radius)
+    products = [first_square]
+    imaged = set()
+    early = []
     k = 0
-    earlier = {}
     for phase, depth in enumerate(PLAN):
         more = phase + 1 < len(PLAN)
         ahead = PLAN[phase + 1] - 1 if more else 0
         if phase == 0:
-            recurrence = lanczos(take_row(0, len(products)))
+            recurrence = lanczos(take_row(0, local_count))
         for step in range(depth):
             if k + step < ADAPTIVE:
                 continue
-            gamma = radius / 2 if step or depth <= 2 else None
-            beta = radius if gamma is None else radius / 2
-            recurrence.append((center, gamma, beta, 1.0 / beta))
+            recurrence.append(usual if step else restart)
         for o, copy in arrivals_of(phase):
             pl.when(there[o])(copy.wait)
+        slots = phase_slots(phase)
+
+        def taken(o):
+            return [
+                jnp.where(there[o], halos[phase, place[o], offset_of(phase, o[1]) + i], 0.0)
+                for i in range(items_of(phase, o))
+            ]
+
+        def beside(got, page_slots, number):
+            return [
+                add([unpack(got[b], page_slots[i], b > 0) for b in got]) for i in range(number)
+            ]
+
+        pots = {(0, 0): fields[k][0]}
+        levels = {(0, 0): tops(k, depth + ahead)}
+        vols = [jnp.where(sub == middle, fields[k][1], zero), zero]
+        for a in range(-deepest, deepest + 1):
+            if (a, 0) in around and around[a, 0] <= depth:
+                got = taken((a, 0))
+                pots[a, 0] = got[0]
+                vols[0] = jnp.where(sub == middle + a, got[1], vols[0])
+                levels[a, 0] = got[2:]
+            if (a, 1) in around and around[a, 1] <= depth:
+                got = {b: taken((a, b)) for b in (-1, 1)}
+                got = beside(got, slots, 2 + depth - around[a, 1])
+                pots[a, 1] = got[0]
+                vols[1] = jnp.where(sub == middle + a, got[1], vols[1])
+                levels[a, 1] = got[2:]
         if phase == 0:
             fixed = {(0, 0): (exch, slope, diff)}
-            for o, _, wait in fixed_moves:
-                pl.when(there[o])(wait.wait)
-            for o, _, _ in fixed_moves:
-                number = 3 if around[o] <= deepest - 2 else 2
-                got = [
-                    jnp.where(there[o], fixed_halos[place[o], i], 0.0)
-                    for i in range(fixed_items_of(o))
-                ]
-                if o[1]:
-                    got = [unpack(got, fixed_slots[i], o[1] > 0) for i in range(number)]
-                fixed[o] = tuple(got)
-        now = {(0, 0): fields[k]}
-        levels = {(0, 0): tops(k, depth + ahead)}
-        before = {(0, 0): tops(k - 1, depth + ahead - 1) if k else None}
-        for o in order:
-            if around[o] <= depth:
-                number = 2 + depth - around[o]
-                got = [
-                    jnp.where(there[o], halos[phase, place[o], i], 0.0)
-                    for i in range(items_of(phase, o))
-                ]
-                if o[1]:
-                    slots = phase_slots(phase)
-                    got = [unpack(got, slots[i], o[1] > 0) for i in range(number)]
-                now[o] = tuple(got[:2])
-                levels[o] = got[2:]
-                before[o] = None
+            exists = {(0, 0): 1.0}
+            exist_vols = [jnp.where(sub == middle, 1.0, zero), zero]
+            for a in range(-deepest, deepest + 1):
+                if (a, 0) in around and around[a, 0] < deepest:
+                    kinds = (1, 2, 0) if around[a, 0] <= deepest - 2 else (1, 2)
+                    fixed[a, 0] = tuple(
+                        jnp.where(there[a, 0], halos[0, place[a, 0], i], 0.0) for i in kinds
+                    )
+                    exists[a, 0] = jnp.where(there[a, 0], 1.0, zero)
+                    exist_vols[0] = jnp.where(sub == middle + a, exists[a, 0], exist_vols[0])
+                if (a, 1) in around and around[a, 1] < deepest:
+                    number = 3 if around[a, 1] <= deepest - 2 else 2
+                    got = {
+                        b: [jnp.where(there[a, b], halos[0, place[a, b], 0], 0.0)]
+                        for b in (-1, 1)
+                    }
+                    fixed[a, 1] = tuple(beside(got, fixed_slots, number))
+                    exists[a, 1] = jnp.where(
+                        cell_y < cy // 2,
+                        jnp.where(there[a, 1], 1.0, zero),
+                        jnp.where(there[a, -1], 1.0, zero),
+                    )
+                    exist_vols[1] = jnp.where(sub == middle + a, exists[a, 1], exist_vols[1])
+        before = {o: None for o in levels}
+        past_pots, past_vols = {}, [None, None]
         currents = []
-        past = earlier
-        if k:
-            past = dict(earlier)
-            past[0, 0] = fields[k - 1]
         for step in range(depth):
             terms = recurrence[k + step]
             reach = depth - step - 1
-            new, new_levels = {}, {}
-            for o in now:
-                if o != (0, 0) and around[o] > reach:
-                    continue
-                near = {
-                    side: now.get((o[0] + side[0], o[1] + side[1])) for side in nowhere
-                }
-                new_p, new_v, current = pots_image(now[o], near, levels[o][0], fixed[o])
-                last = past.get(o, (None, None))
-                p = relate(new_p, now[o][0], last[0], terms)
-                v = relate(new_v, now[o][1], last[1], terms)
-                if o != (0, 0):
-                    p = jnp.where(there[o], p, 0.0)
-                    v = jnp.where(there[o], v, 0.0)
+            todo = [o for o in pots if o == (0, 0) or around[o] <= reach]
+            rolled = {}
+
+            def rolled_pots(o, shift):
+                if o not in pots:
+                    return zero
+                if (o, shift) not in rolled:
+                    rolled[o, shift] = roll(pots[o], shift)
+                return rolled[o, shift]
+
+            def rolled_vols(b, shift):
+                if ("v", b, shift) not in rolled:
+                    rolled["v", b, shift] = roll(vols[b], shift)
+                return rolled["v", b, shift]
+
+            wide = (cx - 1) * cy
+            new_pots, new_levels, sums = {}, {}, [zero, zero]
+            for o in todo:
+                a, b = o
+                p = pots[o]
+                across = jnp.where(
+                    low_x, rolled_pots((a - 1, b), -wide), rolled_pots(o, cy)
+                ) + jnp.where(high_x, rolled_pots((a + 1, b), wide), rolled_pots(o, -cy))
+                other = (a, 1 - b)
+                along = jnp.where(
+                    low_y, rolled_pots(other, 1 - cy), rolled_pots(o, 1)
+                ) + jnp.where(high_y, rolled_pots(other, cy - 1), rolled_pots(o, -1))
+                near_vol = jnp.broadcast_to(
+                    vols[b][middle + a : middle + a + 1, :], (subs, LANES)
+                )
+                current = fixed[o][0] * (p - near_vol)
+                total = current
+                shift = subs // 2
+                while shift:
+                    total = total + roll(total, shift, 0)
+                    shift //= 2
+                sums[b] = jnp.where(sub == middle + a, total, sums[b])
+                image = (
+                    node_cond * node_mirror(p)
+                    + current
+                    - fixed[o][1] * levels[o][0]
+                    + plane_cond * (4.0 * p - (across + along))
+                )
+                value = relate(image, p, past_pots.get(o), terms)
+                if o == (0, 0):
+                    currents.append(current)
                 else:
-                    currents.append(current)
-                new[o] = (p, v)
-                if len(levels[o]) > 1:
-                    new_levels[o] = shell_images(
-                        levels[o], before[o], current, fixed[o][2], terms
-                    )
-                else:
-                    new_levels[o] = []
-            past, now = now, new
-            before, levels = levels, new_levels
-            fields[k + step + 1] = now[0, 0]
-        earlier = {o: f for o, f in past.items() if o != (0, 0)}
+                    value = value * exists[o]
+                new_pots[o] = value
+                new_levels[o] = (
+                    shell_images(levels[o], before[o], current, fixed[o][2], terms)
+                    if len(levels[o]) > 1
+                    else []
+                )
+            new_vols = []
+            for b in range(2):
+                across = jnp.where(
+                    low_x, roll(rolled_vols(b, -wide), 1, 0), rolled_vols(b, cy)
+                ) + jnp.where(high_x, roll(rolled_vols(b, wide), -1, 0), rolled_vols(b, -cy))
+                along = jnp.where(
+                    low_y, rolled_vols(1 - b, 1 - cy), rolled_vols(b, 1)
+                ) + jnp.where(high_y, rolled_vols(1 - b, cy - 1), rolled_vols(b, -1))
+                mean = add([sums[b]] + [roll(sums[b], g * cells) for g in range(1, groups)])
+                image = collector_cond * (4.0 * vols[b] - (across + along)) - mean * (1.0 / nodes)
+                new_vols.append(relate(image, vols[b], past_vols[b], terms) * exist_vols[b])
+            past_pots, past_vols, before = pots, vols, levels
+            pots, vols, levels = new_pots, new_vols, new_levels
+            fields[k + step + 1] = (
+                pots[0, 0],
+                jnp.broadcast_to(vols[0][middle : middle + 1, :], (subs, LANES)),
+            )
         if more:
             send_edges(phase + 1, fields[k + depth], levels[0, 0])
         for step in range(depth):
-            products = full_image(k + step, currents[step], recurrence[k + step], fields)
-            row = row + line_up(products, at)
-            at += len(products)
+            if k + step not in imaged:
+                products += image_shells(
+                    k + step, currents[step], recurrence[k + step], not more
+                )
+            products_pots = pots_products(k + step, fields)
+            base = len(products) - len(products_pots)
+            products[base:] = [c + o for c, o in zip(products[base:], products_pots)]
+        send_row(phase + 1, line_up(products, 0))
+        at = len(products)
+        if more:
+            early_count, early_size = at, k + depth + 1
+            products = image_shells(
+                k + depth,
+                exch * (fields[k + depth][0] - fields[k + depth][1]),
+                restart,
+            )
+            imaged = {k + depth}
         k += depth
-    send_row(1, row)
-    gram = symmetric(take_row(1, at), ITERS + 1)
-    upper, inverse = factor(gram)
-    images = project(upper, inverse, [(a, g, b) for a, g, b, _ in recurrence])
-    start, vectors, columns = arnoldi(upper, inverse, images, ITERS)
-    weights = expand(least_squares(columns, start), vectors, upper, inverse)
+    bases = [r[:3] for r in recurrence]
+    upper, inverse, images, vectors = [], [], [], []
+    target, cosines, sines, uppers = [], [], [], []
+
+    assert len(PLAN) == 2
+
+    def solve_columns(first, last, gram):
+        for j in range(first, last):
+            factor_column(gram, upper, inverse)
+            if j == 0:
+                height = jnp.sqrt(gram[0][0] + epsilon)
+                target.append(height)
+                vectors.append([upper[0][0] / height])
+            else:
+                project_column(upper, inverse, bases, images)
+                entries = arnoldi_column(images, vectors)
+                rotate_column(entries, target, cosines, sines, uppers)
+
+    early += take_row(1, early_count)
+    gram = symmetric(early, early_size)
+    solve_columns(0, early_size, gram)
+    gram = symmetric(early + take_row(len(PLAN), at), ITERS + 1)
+    solve_columns(early_size, ITERS + 1, gram)
+    weights = expand(back_substitute(target, uppers), vectors, upper, inverse)
 
     sol_p = add([w * f[0] for w, f in zip(weights, fields)])
     sol_v = add([w * f[1] for w, f in zip(weights, fields)])
 
-    def gather(c, carry):
-        at = c * CHUNK
-        parts = [weights[i][None] * basis[i, pl.ds(at + 1, CHUNK)] for i in range(ITERS)]
-        basis[ITERS, pl.ds(at + 1, CHUNK)] = add(parts)
-        return carry
-
-    lax.fori_loop(0, shells // CHUNK, gather, 0)
-    flat = jnp.concatenate([basis[ITERS, 1 : shells + 1, s, :] for s in range(subs)], axis=0)
+    mixed = [
+        add([weights[i][None] * basis[i, pl.ds(c * CHUNK + 1, CHUNK)] for i in range(ITERS)])
+        for c in range(shells // CHUNK)
+    ]
+    mixed = jnp.concatenate(mixed, axis=0)
+    flat = jnp.concatenate([mixed[:, s, :] for s in range(subs)], axis=0)
     sol_turned_ref[...] = flat.T
     flat_p = jnp.concatenate(
         [sol_p[:, g * cells : (g + 1) * cells] for g in range(groups)] + [sol_v[:1, :cells]], axis=0
@@ -726,9 +805,7 @@
     for phase in range(len(PLAN)):
         for o, copy in copies_of(phase):
             pl.when(there[o])(copy.wait_send)
-    for o, copy, _ in fixed_moves:
-        pl.when(there[o])(copy.wait_send)
-    for step in range(2):
+    for step in range(len(PLAN) + 1):
         part = rows.at[step, pl.ds(0, count - 1)]
         pltpu.make_async_copy(part, part, row_send.at[step]).wait()
 
@@ -791,20 +868,15 @@
                 pltpu.VMEM((ITERS + 1, shells + 2, subs, LANES), jnp.float32),
                 pltpu.VMEM(rhs_pots.shape, jnp.float32),
                 pltpu.VMEM((3,) + exchange.shape, jnp.float32),
-                pltpu.VMEM((phases, deepest + 1, subs, LANES), jnp.float32),
-                pltpu.VMEM((phases, 2, pages, subs, LANES), jnp.float32),
-                pltpu.VMEM((phases, near, deepest + 1, subs, LANES), jnp.float32),
-                pltpu.VMEM((3, subs, LANES), jnp.float32),
-                pltpu.VMEM((2, pages, subs, LANES), jnp.float32),
-                pltpu.VMEM((near, 3, subs, LANES), jnp.float32),
-                pltpu.VMEM((2, count, 1, LANES), jnp.float32),
-                pltpu.VMEM((2, 1, LANES), jnp.float32),
+                pltpu.VMEM((phases, deepest + 4, subs, LANES), jnp.float32),
+                pltpu.VMEM((phases, 2, pages + 1, subs, LANES), jnp.float32),
+                pltpu.VMEM((phases, near, deepest + 4, subs, LANES), jnp.float32),
+                pltpu.VMEM((phases + 1, count, 1, LANES), jnp.float32),
+                pltpu.VMEM((phases + 1, 1, LANES), jnp.float32),
                 dma((phases, near)),
                 dma((phases, near)),
-                dma((near,)),
-                dma((near,)),
-                dma((2,)),
-                dma((2,)),
+                dma((phases + 1,)),
+                dma((phases + 1,)),
                 dma((cx, groups)),
                 dma((4,)),
             ],

time: 27.1 us -> 25.1 us (0.926)
  Pallas kernels: 26.2 us -> 24.3 us
    pallas_call x1, Pallas kernels: 25.5 us -> 23.5 us  [shards(): pl.pallas_call(functools.partial(cycle, sizes), out_shape=(jax.ShapeDtype...]
where the time goes in v4:
time: 25.1 us; the launch traced here: 24.9 us
  Pallas kernels  24.3 us (97%)
  between operations  0.64 us (3%)
    pallas_call x1, Pallas kernels, shards(): pl.pallas_call(functools.partial(cycle, sizes), out_shape=(jax.ShapeDtype...  23.5 us
    pallas_call x1, Pallas kernels, shards(): pl.pallas_call(place_outputs, out_shape=(jax.ShapeDtypeStruct(rhs_conc.sh...  0.78 us

profile of v4, /device:TPU:0, one launch (start us, length us, event | category | flops | bytes accessed | tf_op | source)
XLA Modules:
  0.0 24.9 jit_solution(9250167503193127082)
XLA Ops:
  0.6 23.5 %shard_map.68 = (f32[128,512]{1,0:T(8,128)S(1)}, f32[2,16,33]{2,1,0:T(8,128)S(1)}) custom-call(f32[2,16,2048]{2,1,0:T(8,128)} %conc_ref.1, f32[2,16,33]{2,1,0:T(8,128)} %pots_ref.1, f32[2,16,32]{2,1,0:T(8,128)} %diff_ref.1, f32[2,16,32]{2,1,0:T(8,128)} %exch_ref.1, f32[2,16,32]{2,1,0:T(8,128)} %slope_ref.1), custom_call_target="tpu_custom_call" | custom-call | tf_op jit(solution)/shard_map/pallas_call | solution.py:858
  24.2 0.8 %shard_map.69 = (f32[2,16,2048]{2,1,0:T(8,128)}, f32[2,16,33]{2,1,0:T(8,128)}) custom-call(f32[128,512]{1,0:T(8,128)S(1)} %get-tuple-element.4.flat_ref, f32[2,16,33]{2,1,0:T(8,128)S(1)} %get-tuple-element.5.pots_ref), custom_call_target="tpu_custom_call" | custom-call | tf_op jit(solution)/shard_map/pallas_call | solution.py:889

commit v5 on v4

--- a/solution.py
+++ b/solution.py
@@ -9,7 +9,7 @@
 
 ITERS = 10
 LANES = 128
-CHUNK = 16
+CHUNK = 32
 PLAN = (5, 5)
 ADAPTIVE = 2
 

time: 25.1 us -> 25.2 us (level)
  no operation moved by 1% of the time
where the time goes in v5:
time: 25.2 us; the launch traced here: 25 us
  Pallas kernels  24.3 us (96%)
  between operations  0.64 us (3%)
    pallas_call x1, Pallas kernels, shards(): pl.pallas_call(functools.partial(cycle, sizes), out_shape=(jax.ShapeDtype...  23.6 us
    pallas_call x1, Pallas kernels, shards(): pl.pallas_call(place_outputs, out_shape=(jax.ShapeDtypeStruct(rhs_conc.sh...  0.78 us

profile of v5, /device:TPU:0, one launch (start us, length us, event | category | flops | bytes accessed | tf_op | source)
XLA Modules:
  0.0 25.0 jit_solution(9743698353163078363)
XLA Ops:
  0.6 23.6 %shard_map.68 = (f32[128,512]{1,0:T(8,128)S(1)}, f32[2,16,33]{2,1,0:T(8,128)S(1)}) custom-call(f32[2,16,2048]{2,1,0:T(8,128)} %conc_ref.1, f32[2,16,33]{2,1,0:T(8,128)} %pots_ref.1, f32[2,16,32]{2,1,0:T(8,128)} %diff_ref.1, f32[2,16,32]{2,1,0:T(8,128)} %exch_ref.1, f32[2,16,32]{2,1,0:T(8,128)} %slope_ref.1), custom_call_target="tpu_custom_call" | custom-call | tf_op jit(solution)/shard_map/pallas_call | solution.py:858
  24.2 0.8 %shard_map.69 = (f32[2,16,2048]{2,1,0:T(8,128)}, f32[2,16,33]{2,1,0:T(8,128)}) custom-call(f32[128,512]{1,0:T(8,128)S(1)} %get-tuple-element.4.flat_ref, f32[2,16,33]{2,1,0:T(8,128)S(1)} %get-tuple-element.5.pots_ref), custom_call_target="tpu_custom_call" | custom-call | tf_op jit(solution)/shard_map/pallas_call | solution.py:889
